TPU v7x, 8 devices: a whole 2x2x1 slice. The times are simulated.
8 devices in a mesh: dp: 1 (over z), ty: 2 (over y), tx: 4 (over x, core).
Axes of the slice: x: 2, y: 2, z: 1, core: 2. Of those that a mesh axis runs over, the one named last changes fastest.
Arguments:
- x_in: bfloat16 [2, 64, 5120], P(('dp', 'ty'), None, 'tx')
- w_q: bfloat16 [5120, 5120], P('tx', 'ty')
- w_k: bfloat16 [5120, 5120], P('tx', 'ty')
- w_v: bfloat16 [5120, 5120], P('tx', 'ty')
- w_o: bfloat16 [5120, 5120], P('ty', 'tx')
- w_gate: bfloat16 [5120, 13824], P('tx', 'ty')
- w_up: bfloat16 [5120, 13824], P('tx', 'ty')
- w_down: bfloat16 [13824, 5120], P('ty', 'tx')
Outputs:
- output: bfloat16 [2, 64, 5120], P(('dp', 'ty'), None, 'tx')
All inputs are finite; a program needn't handle non-finite values.
Results may differ from a plain program's by a relative error of at most 0.0197486.
Values are sent between devices in bfloat16 or wider.
A program may use at most 1 GiB of HBM per device.

v0:
```python
import jax
import jax.numpy as jnp
from jax import lax
from jax.sharding import PartitionSpec as P, NamedSharding

HEAD_DIM = 128
EPS = 1e-5
THETA = 10000.0


def rotary(heads_bf):
    seq_len = heads_bf.shape[1]
    half_dim = HEAD_DIM // 2
    inv_freq = THETA ** (-2.0 * jnp.arange(half_dim, dtype=jnp.float32) / HEAD_DIM)
    angles = jnp.arange(seq_len, dtype=jnp.float32)[:, None] * inv_freq[None, :]
    cos_t = jnp.cos(angles)[:, None, :]
    sin_t = jnp.sin(angles)[:, None, :]
    values = heads_bf.astype(jnp.float32)
    lower_half = values[..., :half_dim]
    upper_half = values[..., half_dim:]
    return jnp.concatenate([lower_half * cos_t - upper_half * sin_t, upper_half * cos_t + lower_half * sin_t], axis=-1).astype(jnp.bfloat16)


def causal_attention(q_heads, k_heads, v_heads):
    seq_len = q_heads.shape[1]
    q_block = min(seq_len, 128)
    key_pos = jnp.arange(seq_len)
    scale_qk = HEAD_DIM ** -0.5

    def one_block(block_idx, out_acc):
        q_start = block_idx * q_block
        q_blk = lax.dynamic_slice_in_dim(q_heads, q_start, q_block, axis=1)
        scores = jnp.einsum("nqhd,nkhd->nhqk", q_blk, k_heads, preferred_element_type=jnp.float32) * scale_qk
        q_pos = q_start + jnp.arange(q_block)
        allowed = q_pos[:, None] >= key_pos[None, :]
        scores = jnp.where(allowed, scores, -1e30)
        prob_blk = jax.nn.softmax(scores, axis=-1).astype(jnp.bfloat16)
        blk_out = jnp.einsum("nhqk,nkhd->nqhd", prob_blk, v_heads, preferred_element_type=jnp.float32).astype(jnp.bfloat16)
        return lax.dynamic_update_slice_in_dim(out_acc, blk_out, q_start, axis=1)

    return lax.fori_loop(0, seq_len // q_block, one_block, jnp.zeros_like(q_heads))


def norm_sharded(values_bf, full_width):
    values = values_bf.astype(jnp.float32)
    moments = jnp.stack([jnp.sum(values, axis=-1), jnp.sum(values * values, axis=-1)], axis=-1)
    moments = lax.psum(moments, "tx")
    mean_val = moments[..., 0:1] / full_width
    var_val = moments[..., 1:2] / full_width - mean_val * mean_val
    return ((values - mean_val) * lax.rsqrt(var_val + EPS)).astype(jnp.bfloat16)


def project(rows_bf, weight):
    return jnp.einsum("...c,ch->...h", rows_bf, weight, preferred_element_type=jnp.float32).astype(jnp.bfloat16)


def solution(mesh):
    tx_count = mesh.shape["tx"]
    act_spec = P(("dp", "ty"), None, "tx")
    col_spec = P("tx", "ty")
    row_spec = P("ty", "tx")

    def layer_fn(x_blk, w_q, w_k, w_v, w_o, w_gate, w_up, w_down):
        full_width = x_blk.shape[-1] * tx_count
        normed_all = lax.all_gather(norm_sharded(x_blk, full_width), "ty", axis=0, tiled=True)
        q_sum, k_sum, v_sum = lax.psum((project(normed_all, w_q), project(normed_all, w_k), project(normed_all, w_v)), "tx")
        n_seqs, seq_len, local_cols = q_sum.shape
        head_shape = (n_seqs, seq_len, local_cols // HEAD_DIM, HEAD_DIM)
        attn_heads = causal_attention(rotary(q_sum.reshape(head_shape)), rotary(k_sum.reshape(head_shape)), v_sum.reshape(head_shape))
        attn_out = lax.psum_scatter(project(attn_heads.reshape(q_sum.shape), w_o), "ty", scatter_dimension=0, tiled=True)
        resid_h = (x_blk.astype(jnp.float32) + attn_out.astype(jnp.float32)).astype(jnp.bfloat16)
        normed_mlp = lax.all_gather(norm_sharded(resid_h, full_width), "ty", axis=0, tiled=True)
        gate_sum, up_sum = lax.psum((project(normed_mlp, w_gate), project(normed_mlp, w_up)), "tx")
        act_val = (jax.nn.silu(gate_sum.astype(jnp.float32)) * up_sum.astype(jnp.float32)).astype(jnp.bfloat16)
        mlp_out = lax.psum_scatter(project(act_val, w_down), "ty", scatter_dimension=0, tiled=True)
        return (resid_h.astype(jnp.float32) + mlp_out.astype(jnp.float32)).astype(jnp.bfloat16)

    return jax.shard_map(layer_fn, mesh=mesh, in_specs=(act_spec, col_spec, col_spec, col_spec, row_spec, col_spec, col_spec, row_spec), out_specs=act_spec, check_vma=False)
```

profile of v0, /device:TPU:0, one launch (start us, length us, event | category | flops | bytes accessed | tf_op | source)
XLA Modules:
  0.0 231.2 jit_solution(7750453039463321410)
XLA Ops:
  6.5 1.1 convert_reduce_fusion.1
  7.6 8.8 %psum.49 = f32[1,64,2]{1,2,0:T(2,128)S(1)} all-reduce(f32[1,64,2]{1,2,0:T(2,128)S(1)} %pad_maximum_fusion), channel_id=1, replica_groups=mesh['dp'=1,'ty'=2,'tx'=4] {'tx'}, use_global_device_ids=true, to_apply=%region_2.0 | all-reduce | flops 128 | bytes 1024 | tf_op jit(solution)/shard_map/psum | solution.py:47
  17.4 6.0 %all_gather.6 = bf16[2,64,1280]{2,1,0:T(8,128)(2,1)S(1)} all-gather(bf16[1,64,1280]{2,1,0:T(8,128)(2,1)S(1)} %fusion.67), channel_id=1, replica_groups=mesh['dp'=1,'ty'=2,'tx'=4] {'ty'}, dimensions={0}, use_global_device_ids=true | all-gather | bytes 491520 | tf_op jit(solution)/shard_map/all_gather | solution.py:65
  23.4 4.0 %fusion.47 = bf16[2,8,20,8,128]{4,3,2,1,0:T(8,128)(2,1)S(1)} fusion(bf16[2,64,1280]{2,1,0:T(8,128)(2,1)S(1)} %all_gather.6, bf16[1280,2560]{1,0:T(8,128)(2,1)} %param.10), kind=kOutput, calls=%fused_computation.41 | convolution fusion | flops 839188480 | bytes 7536640 | tf_op jit(solution)/shard_map/...c,ch->...h/dot_general | solution.py:54
  28.1 1.0 fusion.50
  29.2 1.8 copy-done.1
  31.0 1.0 fusion.53
  32.0 1.0 copy.35
  33.1 1.5 copy_bitcast_fusion
  34.8 43.9 %all-reduce.7.cloned.1.call-done = (bf16[2,64,20,128]{3,1,2,0:T(8,128)(2,1)}, bf16[2,64,20,128]{3,1,2,0:T(8,128)(2,1)}, bf16[2,64,20,128]{3,1,2,0:T(8,128)(2,1)}) async-done(((bf16[2,64,20,128]{3,1,2,0:T(8,128)(2,1)}, bf16[2,64,20,128]{3,1,2,0:T(8,128)(2,1)}, bf16[2,64,20,128]{3,1,2,0:T(8,128)(2,1)}), (bf16[2,64,20,128]{3,1,2,0:T(8,128)(2,1)}, bf16[2,64,20,128]{3,1,2,0:T(8,128)(2,1)}, ...) | async-done | bytes 1966096 | tf_op jit(solution)/shard_map/psum | solution.py:66
  78.7 1.3 convert_element_type.86
  81.2 2.2 fusion.93
  83.3 1.7 fusion.46
  85.0 4.7 %fusion.35 = bf16[2,64,1280]{2,1,0:T(8,128)(2,1)} fusion(bf16[2560,1280]{1,0:T(8,128)(2,1)} %param.12, bf16[2,20,8,8,128]{4,3,2,1,0:T(8,128)(2,1)S(1)} %fusion.46), kind=kOutput, calls=%fused_computation.27 | convolution fusion | flops 839024640 | bytes 7536640 | tf_op jit(solution)/shard_map/...c,ch->...h/dot_general | solution.py:54
  89.8 9.8 %reduce-scatter.3.cloned.1.call-done = bf16[1,64,1280]{2,1,0:T(8,128)(2,1)} async-done(((bf16[2,64,1280]{2,1,0:T(8,128)(2,1)}), bf16[1,64,1280]{2,1,0:T(8,128)(2,1)}) %reduce-scatter.3.cloned.1.call-update) | async-done | bytes 163856 | tf_op jit(solution)/shard_map/reduce_scatter | solution.py:70
  99.6 1.1 convert_reduce_fusion
  100.7 6.3 %psum.53 = f32[1,64,2]{1,2,0:T(2,128)S(1)} all-reduce(f32[1,64,2]{1,2,0:T(2,128)S(1)} %pad_maximum_fusion.1), channel_id=1, replica_groups=mesh['dp'=1,'ty'=2,'tx'=4] {'tx'}, use_global_device_ids=true, to_apply=%region_11.12 | all-reduce | flops 128 | bytes 1024 | tf_op jit(solution)/shard_map/psum | solution.py:47
  107.2 6.2 %all_gather.7 = bf16[2,64,1280]{2,1,0:T(8,128)(2,1)S(1)} all-gather(bf16[1,64,1280]{2,1,0:T(8,128)(2,1)S(1)} %fusion.71), channel_id=1, replica_groups=mesh['dp'=1,'ty'=2,'tx'=4] {'ty'}, dimensions={0}, use_global_device_ids=true | all-gather | bytes 491520 | tf_op jit(solution)/shard_map/all_gather | solution.py:72
  113.3 9.8 %fusion.10 = bf16[2,64,6912]{2,1,0:T(8,128)(2,1)} fusion(bf16[2,64,1280]{2,1,0:T(8,128)(2,1)S(1)} %all_gather.7, bf16[1280,6912]{1,0:T(8,128)(2,1)} %param.14), kind=kOutput, calls=%fused_computation.8 | convolution fusion | flops 2265808896 | bytes 19791872 | tf_op jit(solution)/shard_map/...c,ch->...h/dot_general | solution.py:54
  123.1 9.8 %fusion.7 = bf16[2,64,6912]{2,1,0:T(8,128)(2,1)} fusion(bf16[2,64,1280]{2,1,0:T(8,128)(2,1)S(1)} %all_gather.7, bf16[1280,6912]{1,0:T(8,128)(2,1)} %param.13), kind=kOutput, calls=%fused_computation.7 | convolution fusion | flops 2265808896 | bytes 19791872 | tf_op jit(solution)/shard_map/...c,ch->...h/dot_general | solution.py:54
  133.0 69.2 %all-reduce.5.cloned.1.call-done = (bf16[2,64,6912]{2,1,0:T(8,128)(2,1)}, bf16[2,64,6912]{2,1,0:T(8,128)(2,1)}) async-done(((bf16[2,64,6912]{2,1,0:T(8,128)(2,1)}, bf16[2,64,6912]{2,1,0:T(8,128)(2,1)}), (bf16[2,64,6912]{2,1,0:T(8,128)(2,1)}, bf16[2,64,6912]{2,1,0:T(8,128)(2,1)})) %all-reduce.5.cloned.1.call-update) | async-done | bytes 3538960 | tf_op jit(solution)/shard_map/psum | solution.py:73
  202.3 10.9 %fusion.38 = bf16[2,64,1280]{2,1,0:T(8,128)(2,1)} fusion(bf16[6912,1280]{1,0:T(8,128)(2,1)} %param.15, bf16[2,64,6912]{2,1,0:T(8,128)(2,1)} %get-tuple-element.28, bf16[2,64,6912]{2,1,0:T(8,128)(2,1)} %get-tuple-element.30), kind=kOutput, calls=%fused_computation.28 | convolution fusion | flops 2272165888 | bytes 21561344 | tf_op jit(solution)/shard_map/...c,ch->...h/dot_general | solution.py:54
  213.2 9.9 %reduce-scatter.5.cloned.1.call-done = bf16[1,64,1280]{2,1,0:T(8,128)(2,1)} async-done(((bf16[2,64,1280]{2,1,0:T(8,128)(2,1)}), bf16[1,64,1280]{2,1,0:T(8,128)(2,1)}) %reduce-scatter.5.cloned.1.call-update) | async-done | bytes 163856 | tf_op jit(solution)/shard_map/reduce_scatter | solution.py:75
  223.1 1.6 fusion.72
  (28 shorter events, 3.3 us)
Async XLA Ops:
  6.5 72.2 %all-reduce.7.cloned.1.call-start = ((), (), s32[]{:S(2)}) async-start(), calls=%async_computation.5 | async-start | bytes 3932160 | tf_op jit(solution)/shard_map/psum | solution.py:66
  23.4 4.7 %copy-start = (bf16[1280,2560]{1,0:T(8,128)(2,1)S(1)}, bf16[1280,2560]{1,0:T(8,128)(2,1)}, u32[]{:S(2)}) copy-start(bf16[1280,2560]{1,0:T(8,128)(2,1)} %param.9) | copy-start | bytes 19660804
  28.1 2.9 %copy-start.1 = (bf16[1280,2560]{1,0:T(8,128)(2,1)S(1)}, bf16[1280,2560]{1,0:T(8,128)(2,1)}, u32[]{:S(2)}) copy-start(bf16[1280,2560]{1,0:T(8,128)(2,1)} %param.11) | copy-start | bytes 19660804
  34.5 65.1 %reduce-scatter.3.cloned.1.call-start = ((), (), s32[]{:S(2)}) async-start(), calls=%async_computation.2 | async-start | bytes 491520 | tf_op jit(solution)/shard_map/reduce_scatter | solution.py:70
  78.7 1.3 copy-start.3
  81.1 2.2 copy-start.4
  85.0 14.6 %copy-start.2 = (bf16[1,64,1280]{2,1,0:T(8,128)(2,1)S(1)}, bf16[1,64,1280]{2,1,0:T(8,128)(2,1)}, u32[]{:S(2)}) copy-start(bf16[1,64,1280]{2,1,0:T(8,128)(2,1)} %param.8) | copy-start | bytes 491524
  89.8 112.5 %all-reduce.5.cloned.1.call-start = ((), (), s32[]{:S(2)}) async-start(), calls=%async_computation.4 | async-start | bytes 7077888 | tf_op jit(solution)/shard_map/psum | solution.py:73
  133.0 90.1 %reduce-scatter.5.cloned.1.call-start = ((), (), s32[]{:S(2)}) async-start(), calls=%async_computation.3 | async-start | bytes 491520 | tf_op jit(solution)/shard_map/reduce_scatter | solution.py:75
Sparse Core Ops, SparseCore 0:
  34.7 44.0 all-reduce.6
  89.9 9.6 reduce-scatter.2
  133.1 69.1 all-reduce.4
  213.3 9.7 reduce-scatter.4
where the time goes:
time: 232 us; the launch traced here: 231 us
  waiting for transfers between devices  133 us (57%)
  matrix products  45.2 us (19%)
  blocking collectives  27.2 us (12%)
  between operations  13.3 us (6%)
  other arithmetic  7.49 us (3%)
  local copies, waits for them, and re-layouts  5.02 us (2%)
    psum x1, waiting for transfers between devices, layer_fn(): lax.psum((project(normed_mlp, w_gate), project(normed_mlp, w_up)), 'tx')  69.2 us
    psum x1, waiting for transfers between devices, layer_fn(): lax.psum((project(normed_all, w_q), project(normed_all, w_k), project(nor...  43.9 us
    dot_general x7, matrix products, project(): jnp.einsum('...c,ch->...h', rows_bf, weight, preferred_element_type=jnp.f...  41.3 us
    psum x2, blocking collectives, norm_sharded(): moments = lax.psum(moments, 'tx')  15.1 us
    reduce_scatter x1, waiting for transfers between devices, layer_fn(): lax.psum_scatter(project(act_val, w_down), 'ty', scatter_dimension=0, til...  9.88 us
    reduce_scatter x1, waiting for transfers between devices, layer_fn(): lax.psum_scatter(project(attn_heads.reshape(q_sum.shape), w_o), 'ty', sca...  9.78 us
    all_gather x1, blocking collectives, layer_fn(): lax.all_gather(norm_sharded(resid_h, full_width), 'ty', axis=0, tiled=True)  6.17 us
    all_gather x1, blocking collectives, layer_fn(): lax.all_gather(norm_sharded(x_blk, full_width), 'ty', axis=0, tiled=True)  5.99 us
  transfers between devices with their start and end apart: 4, of which 4 were waited for; matrix products, arithmetic and copies ran while one was open for 0% of the time, Pallas kernels for 0%

commit v1 on v0

v1 whole, which is shorter than its diff:
```python
import functools

import jax
import jax.numpy as jnp
import numpy as np
from jax import lax
from jax.experimental import pallas as pl
from jax.experimental.pallas import tpu as pltpu
from jax.sharding import PartitionSpec as P

HEAD_DIM = 128
EPS = 1e-5
THETA = 10000.0
MESH = pl.DeviceIdType.MESH

S = 64
D1 = 1280
DFULL = 5120
GH = 5
GW = GH * HEAD_DIM
CH = 768
NJ = 9
NU = 2 * NJ
NP = 4
L1, L2, L3, L4 = 1, 3, 5, 6


def rotary_tables():
    half = HEAD_DIM // 2
    inv_freq = np.float32(THETA) ** (np.float32(-2.0) * np.arange(half, dtype=np.float32) / np.float32(HEAD_DIM))
    angles = np.arange(S, dtype=np.float32)[:, None] * inv_freq.astype(np.float32)[None, :]
    cos_t = np.cos(angles.astype(np.float64)).astype(np.float32)
    sin_t = np.sin(angles.astype(np.float64)).astype(np.float32)
    return np.concatenate([cos_t, cos_t], axis=1), np.concatenate([-sin_t, sin_t], axis=1)


def bdot(a, b):
    return jnp.dot(a, b, preferred_element_type=jnp.float32)


def kernel(
    x_hbm, wq, wk, wv, wo, wg, wu, wd, cos_hbm, sin_hbm, y_hbm,
    WA, WB, XB, NB, HB, ST1, ST2, PS, PO, R1, XS, R2, OF, AO, AR,
    MP, MR1, MXS, MR2, AF, ACC, DS, DR, COS, SIN, YB,
    wsem, lsem, xg_s, xg_r, st1_s, st1_r, st2_s, st2_r,
    q1_s, q1_r, q2_s, q2_r, ox_s, ox_r, od_s, od_r, ay_s, ay_r,
    m1_s, m1_r, m2_s, m2_r, ax_s, ax_r, ad_s, ad_r, dy_s, dy_r,
):
    f32, bf16 = jnp.float32, jnp.bfloat16
    ty = lax.axis_index("ty")
    tx = lax.axis_index("tx")
    c = lax.rem(tx, 2)
    xx = lax.div(tx, 2)
    co, xo = 1 - c, 1 - xx
    tyo = 1 - ty
    partner = {"tx": 2 * xx + co}
    xpeer = {"tx": 2 * xo + c}
    ypeer = {"ty": tyo}

    def rcopy(src, dst, ss, rs, dev):
        return pltpu.make_async_remote_copy(src_ref=src, dst_ref=dst, send_sem=ss, recv_sem=rs, device_id=dev, device_id_type=MESH)

    x_load = pltpu.make_async_copy(x_hbm, XB.at[0], lsem.at[0])
    x_load.start()
    cos_load = pltpu.make_async_copy(cos_hbm, COS, lsem.at[1])
    sin_load = pltpu.make_async_copy(sin_hbm, SIN, lsem.at[2])

    barrier = pltpu.get_barrier_semaphore()
    for k in range(1, 4):
        pl.semaphore_signal(barrier, inc=1, device_id={"tx": lax.rem(tx + k, 4)}, device_id_type=MESH)
    for k in range(4):
        pl.semaphore_signal(barrier, inc=1, device_id={"ty": tyo, "tx": lax.rem(tx + k, 4)}, device_id_type=MESH)

    def qkv_load(m, half):
        src = (wq, wk, wv)[m].at[:, pl.ds(half * D1, D1)]
        return pltpu.make_async_copy(src, WB.at[pl.ds((2 * m + half) * D1, D1), :], wsem.at[2 * m + half])

    def wo_load(i):
        kh, wide = i % 2, i // 2
        if wide == 0:
            return pltpu.make_async_copy(wo.at[pl.ds(kh * D1, D1), pl.ds(0, CH)], WA.at[14 + i], wsem.at[6 + i])
        return pltpu.make_async_copy(wo.at[pl.ds(kh * D1, D1), pl.ds(CH, D1 - CH)], WA.at[14 + i, :, pl.ds(0, D1 - CH)], wsem.at[6 + i])

    def gu_load(j, which):
        off = pl.multiple_of(j * CH, CH)
        return pltpu.make_async_copy((wg, wu)[which].at[:, pl.ds(off, CH)], WA.at[2 * j + which], wsem.at[10 + 2 * j + which])

    def wd_load(j):
        off = pl.multiple_of(j * CH, CH)
        return pltpu.make_async_copy(wd.at[pl.ds(off, CH), :], WB.at[pl.ds(off, CH), :], wsem.at[28 + j])

    for m in range(3):
        for half in range(2):
            qkv_load(m, half).start()
    cos_load.start()
    sin_load.start()
    for i in range(4):
        wo_load(i).start()
    for j in range(7):
        gu_load(j, 0).start()
        gu_load(j, 1).start()

    eye = lax.broadcasted_iota(jnp.int32, (S, 128), 0) == lax.broadcasted_iota(jnp.int32, (S, 128), 1)
    row8 = lax.broadcasted_iota(jnp.int32, (8, 128), 0)

    def stats_tile(v):
        s = jnp.sum(v, axis=1, keepdims=True)
        q = jnp.sum(v * v, axis=1, keepdims=True)
        srow = jnp.sum(jnp.where(eye, s, 0.0), axis=0, keepdims=True)
        qrow = jnp.sum(jnp.where(eye, q, 0.0), axis=0, keepdims=True)
        return jnp.where(row8 == 0, srow, jnp.where(row8 == 1, qrow, 0.0))

    def normalize(v, tot):
        mean = tot[0:1, :] / DFULL
        var = tot[1:2, :] / DFULL - mean * mean
        rstd = lax.rsqrt(var + EPS)
        mean_c = jnp.sum(jnp.where(eye, mean, 0.0), axis=1, keepdims=True)
        rstd_c = jnp.sum(jnp.where(eye, rstd, 0.0), axis=1, keepdims=True)
        return ((v - mean_c) * rstd_c).astype(bf16)

    x_load.wait()
    x_own = XB[0].astype(f32)
    ST1[0, 0] = stats_tile(x_own)
    pl.semaphore_wait(barrier, 7)

    def st1_copy(r, k):
        dev = {"tx": lax.rem(tx + k, 4)} if r == 0 else {"ty": tyo, "tx": lax.rem(tx + k, 4)}
        return rcopy(ST1.at[0, 0], ST1.at[r, k], st1_s.at[r, k], st1_r.at[r, k], dev)

    for k in range(1, 4):
        st1_copy(0, k).start()
    x_send = rcopy(XB.at[0], XB.at[1], xg_s.at[0], xg_r.at[0], ypeer)
    x_send.start()
    for k in range(4):
        st1_copy(1, k).start()

    def q1_copy(r, m):
        return rcopy(PS.at[r, m], R1.at[r, m], q1_s.at[r, m], q1_r.at[r, m], partner)

    def q2_copy(r, m):
        return rcopy(XS.at[r, m], R2.at[r, m], q2_s.at[r, m], q2_r.at[r, m], xpeer)

    def qkv_mm(r, m):
        if r == 0:
            qkv_load(m, 0).wait()
            qkv_load(m, 1).wait()
        n = NB[r]
        for which in range(2):
            half = co if which == 0 else c
            dst = PS if which == 0 else PO
            res = bdot(n, WB[pl.ds(pl.multiple_of((2 * m + half) * D1, D1), D1), :]).astype(bf16)
            dst[r, m, 0] = res[:, :GW]
            dst[r, m, 1] = res[:, GW:]
            if which == 0:
                q1_copy(r, m).start()

    def qkv_s1(r, m):
        q1_copy(r, m).wait_recv()
        XS[r, m] = (PO[r, m, xo].astype(f32) + R1[r, m, xo].astype(f32)).astype(bf16)
        q2_copy(r, m).start()

    for k in range(1, 4):
        st1_copy(0, k).wait_recv()
    NB[0] = normalize(x_own, ST1[0, 0] + ST1[0, 1] + ST1[0, 2] + ST1[0, 3])
    qkv_mm(0, 0)
    qkv_mm(0, 1)
    qkv_s1(0, 0)
    qkv_mm(0, 2)
    qkv_s1(0, 1)

    x_send.wait_recv()
    for k in range(4):
        st1_copy(1, k).wait_recv()
    NB[1] = normalize(XB[1].astype(f32), ST1[1, 0] + ST1[1, 1] + ST1[1, 2] + ST1[1, 3])
    qkv_mm(1, 0)
    qkv_s1(0, 2)
    qkv_mm(1, 1)
    qkv_s1(1, 0)
    qkv_mm(1, 2)
    for j in range(NJ):
        wd_load(j).start()
    qkv_s1(1, 1)
    qkv_s1(1, 2)

    cos_load.wait()
    sin_load.wait()
    causal = lax.broadcasted_iota(jnp.int32, (S, S), 0) >= lax.broadcasted_iota(jnp.int32, (S, S), 1)

    def ox_copy(r):
        return rcopy(OF.at[r, c, xx], OF.at[r, c, xx], ox_s.at[r], ox_r.at[r], xpeer)

    def ox_recv(r):
        return rcopy(OF.at[r, c, xo], OF.at[r, c, xo], ox_s.at[r], ox_r.at[r], xpeer)

    def od_copy(r):
        return rcopy(OF.at[r, c], OF.at[r, c], od_s.at[r], od_r.at[r], partner)

    def od_recv(r):
        return rcopy(OF.at[r, co], OF.at[r, co], od_s.at[r], od_r.at[r], partner)

    def attention(r):
        cos_t, sin_t = COS[...], SIN[...]
        full = []
        for m in range(3):
            q2_copy(r, m).wait_recv()
            full.append((PO[r, m, xx].astype(f32) + R1[r, m, xx].astype(f32) + R2[r, m].astype(f32)).astype(bf16))

        def rot(v):
            v = v.astype(f32)
            return (v * cos_t + pltpu.roll(v, HEAD_DIM // 2, 1) * sin_t).astype(bf16)

        outs = []
        for h in range(GH):
            cols = slice(h * HEAD_DIM, (h + 1) * HEAD_DIM)
            qh, kh, vh = rot(full[0][:, cols]), rot(full[1][:, cols]), full[2][:, cols]
            sc = lax.dot_general(qh, kh, (((1,), (1,)), ((), ())), preferred_element_type=f32) * HEAD_DIM ** -0.5
            sc = jnp.where(causal, sc, -1e30)
            e = jnp.exp(sc - jnp.max(sc, axis=1, keepdims=True))
            p = (e / jnp.sum(e, axis=1, keepdims=True)).astype(bf16)
            outs.append(bdot(p, vh).astype(bf16))
        OF[r, c, xx] = jnp.concatenate(outs, axis=1)
        ox_copy(r).start()

    def o_forward(r):
        ox_recv(r).wait_recv()
        od_copy(r).start()

    def ay_copy(r):
        return rcopy(AO.at[r], AR.at[1 - r], ay_s.at[r], ay_r.at[1 - r], ypeer)

    def out_proj(r):
        if r == 0:
            for i in range(4):
                wo_load(i).wait()
        od_recv(r).wait_recv()
        o0 = jnp.concatenate([OF[r, 0, 0], OF[r, 0, 1]], axis=1)
        o1 = jnp.concatenate([OF[r, 1, 0], OF[r, 1, 1]], axis=1)
        AO[r, :, :CH] = (bdot(o0, WA[14]) + bdot(o1, WA[15])).astype(bf16)
        AO[r, :, CH:] = (bdot(o0, WA[16, :, : D1 - CH]) + bdot(o1, WA[17, :, : D1 - CH])).astype(bf16)
        ay_copy(r).start()

    attention(0)
    attention(1)
    o_forward(0)
    out_proj(0)
    o_forward(1)
    out_proj(1)
    for j in range(7, NJ):
        gu_load(j, 0).start()
        gu_load(j, 1).start()

    def st2_copy(r, k):
        return rcopy(ST2.at[r, 0], ST2.at[r, k], st2_s.at[r, k], st2_r.at[r, k], {"tx": lax.rem(tx + k, 4)})

    def residual(r):
        ay_copy(1 - r).wait_recv()
        attn = (AO[r].astype(f32) + AR[r].astype(f32)).astype(bf16)
        h = (XB[r].astype(f32) + attn.astype(f32)).astype(bf16)
        HB[r] = h
        ST2[r, 0] = stats_tile(h.astype(f32))
        for k in range(1, 4):
            st2_copy(r, k).start()

    def norm2(r):
        for k in range(1, 4):
            st2_copy(r, k).wait_recv()
        NB[r] = normalize(HB[r].astype(f32), ST2[r, 0] + ST2[r, 1] + ST2[r, 2] + ST2[r, 3])

    residual(1)
    norm2(1)

    def m1_copy(u, j):
        return rcopy(MP.at[lax.rem(u, NP), pl.ds(2 * co, 2)], MR1.at[j], m1_s.at[j], m1_r.at[j], partner)

    def m2_copy(j):
        return rcopy(MXS.at[j], MR2.at[j], m2_s.at[j], m2_r.at[j], xpeer)

    def ax_copy(j):
        return rcopy(AF.at[j, 2 * c + xx], AF.at[j, 2 * c + xx], ax_s.at[j], ax_r.at[j], xpeer)

    def ax_recv(j):
        return rcopy(AF.at[j, 2 * c + xo], AF.at[j, 2 * c + xo], ax_s.at[j], ax_r.at[j], xpeer)

    def ad_copy(j):
        return rcopy(AF.at[j, pl.ds(2 * c, 2)], AF.at[j, pl.ds(2 * c, 2)], ad_s.at[j], ad_r.at[j], partner)

    def ad_recv(j):
        return rcopy(AF.at[j, pl.ds(2 * co, 2)], AF.at[j, pl.ds(2 * co, 2)], ad_s.at[j], ad_r.at[j], partner)

    def dy_copy():
        return rcopy(DS, DR, dy_s.at[0], dy_r.at[0], ypeer)

    def stage0(u):
        half, j = lax.div(u, NJ), lax.rem(u, NJ)

        @pl.when(u < NJ)
        def _():
            gu_load(j, 0).wait()
            gu_load(j, 1).wait()

        slot = lax.rem(u, NP)
        n = NB[1 - half]
        for which in range(2):
            res = bdot(n, WA[2 * j + which]).astype(bf16)
            for b in range(4):
                MP[slot, b, which] = res[16 * b:16 * (b + 1), :]
        m1_copy(u, j).start()

    def stage1(u):
        j, slot = lax.rem(u, NJ), lax.rem(u, NP)
        m1_copy(u, j).wait_recv()
        MXS[j] = (MP[slot, 2 * c + xo].astype(f32) + MR1[j, xo].astype(f32)).astype(bf16)
        m2_copy(j).start()

    def stage2(u):
        j, slot = lax.rem(u, NJ), lax.rem(u, NP)
        m1_copy(u, j).wait_send()
        m2_copy(j).wait_recv()
        tot = (MP[slot, 2 * c + xx].astype(f32) + MR1[j, xx].astype(f32) + MR2[j].astype(f32)).astype(bf16).astype(f32)
        gate, up = tot[0], tot[1]
        AF[j, 2 * c + xx] = (gate * jax.nn.sigmoid(gate) * up).astype(bf16)
        ax_copy(j).start()

    def stage3(u):
        j = lax.rem(u, NJ)
        m2_copy(j).wait_send()
        ax_recv(j).wait_recv()
        ad_copy(j).start()

    def stage4(u):
        j = lax.rem(u, NJ)
        ax_copy(j).wait_send()

        @pl.when(u < NJ)
        def _():
            wd_load(j).wait()

        ad_recv(j).wait_recv()
        a = jnp.concatenate([AF[j, b] for b in range(4)], axis=0)
        prod = bdot(a, WB[pl.ds(pl.multiple_of(j * CH, CH), CH), :])

        @pl.when(j == 0)
        def _():
            ACC[...] = prod

        @pl.when(j > 0)
        def _():
            ACC[...] += prod

        ad_copy(j).wait_send()

        @pl.when(u == NJ - 1)
        def _():
            DS[...] = ACC[...].astype(bf16)
            dy_copy().start()

    def step(t, carry):
        @pl.when(t == NJ - 3)
        def _():
            residual(0)

        @pl.when(t == NJ)
        def _():
            norm2(0)

        @pl.when(t < NU)
        def _():
            stage0(t)

        for lag, stage in ((L1, stage1), (L2, stage2), (L3, stage3), (L4, stage4)):
            @pl.when((t >= lag) & (t < NU + lag))
            def _(lag=lag, stage=stage):
                stage(t - lag)

        return carry

    lax.fori_loop(0, NU + L4, step, 0)

    dy_copy().wait_recv()
    mlp = (ACC[...] + DR[...].astype(f32)).astype(bf16)
    YB[...] = (HB[0].astype(f32) + mlp.astype(f32)).astype(bf16)
    y_store = pltpu.make_async_copy(YB, y_hbm, lsem.at[0])
    y_store.start()
    for k in range(1, 4):
        st1_copy(0, k).wait_send()
    for k in range(4):
        st1_copy(1, k).wait_send()
    x_send.wait_send()
    for r in range(2):
        for m in range(3):
            q1_copy(r, m).wait_send()
            q2_copy(r, m).wait_send()
        ox_copy(r).wait_send()
        od_copy(r).wait_send()
        ay_copy(r).wait_send()
        for k in range(1, 4):
            st2_copy(r, k).wait_send()
    dy_copy().wait_send()
    y_store.wait()


def layer_fn(x_blk, w_q, w_k, w_v, w_o, w_gate, w_up, w_down):
    bf16, f32 = jnp.bfloat16, jnp.float32
    cos_t, sin_t = rotary_tables()
    vm, dma = pltpu.VMEM, pltpu.SemaphoreType.DMA
    scratch = [
        vm((2 * NJ, D1, CH), bf16),
        vm((6 * D1, D1), bf16),
        vm((2, S, D1), bf16),
        vm((2, S, D1), bf16),
        vm((2, S, D1), bf16),
        vm((2, 4, 8, 128), f32),
        vm((2, 4, 8, 128), f32),
        vm((2, 3, 2, S, GW), bf16),
        vm((2, 3, 2, S, GW), bf16),
        vm((2, 3, 2, S, GW), bf16),
        vm((2, 3, S, GW), bf16),
        vm((2, 3, S, GW), bf16),
        vm((2, 2, 2, S, GW), bf16),
        vm((2, S, D1), bf16),
        vm((2, S, D1), bf16),
        vm((NP, 4, 2, 16, CH), bf16),
        vm((NJ, 2, 2, 16, CH), bf16),
        vm((NJ, 2, 16, CH), bf16),
        vm((NJ, 2, 16, CH), bf16),
        vm((NJ, 4, 16, CH), bf16),
        vm((S, D1), f32),
        vm((S, D1), bf16),
        vm((S, D1), bf16),
        vm((S, HEAD_DIM), f32),
        vm((S, HEAD_DIM), f32),
        vm((S, D1), bf16),
        dma((37,)), dma((3,)), dma((1,)), dma((1,)),
        dma((2, 4)), dma((2, 4)), dma((2, 4)), dma((2, 4)),
        dma((2, 3)), dma((2, 3)), dma((2, 3)), dma((2, 3)),
        dma((2,)), dma((2,)), dma((2,)), dma((2,)), dma((2,)), dma((2,)),
        dma((NJ,)), dma((NJ,)), dma((NJ,)), dma((NJ,)),
        dma((NJ,)), dma((NJ,)), dma((NJ,)), dma((NJ,)), dma((1,)), dma((1,)),
    ]
    y = pl.pallas_call(
        kernel,
        out_shape=jax.ShapeDtypeStruct((S, D1), bf16),
        in_specs=[pl.BlockSpec(memory_space=pl.ANY)] * 10,
        out_specs=pl.BlockSpec(memory_space=pl.ANY),
        scratch_shapes=scratch,
        compiler_params=pltpu.CompilerParams(collective_id=0, has_side_effects=True, vmem_limit_bytes=67_043_328),
    )(x_blk.reshape(S, D1), w_q, w_k, w_v, w_o, w_gate, w_up, w_down, jnp.asarray(cos_t), jnp.asarray(sin_t))
    return y.reshape(x_blk.shape)


def solution(mesh):
    act_spec = P(("dp", "ty"), None, "tx")
    col_spec = P("tx", "ty")
    row_spec = P("ty", "tx")
    return jax.shard_map(
        layer_fn,
        mesh=mesh,
        in_specs=(act_spec, col_spec, col_spec, col_spec, row_spec, col_spec, col_spec, row_spec),
        out_specs=act_spec,
        check_vma=False,
    )
```

time: 232 us -> 74.6 us (0.32)
  waiting for transfers between devices: 133 us -> 0 us
  Pallas kernels: 0 us -> 72.9 us
  matrix products: 45.2 us -> 0 us
  blocking collectives: 27.2 us -> 0 us
  between operations: 13.3 us -> 0.01 us
  other arithmetic: 7.49 us -> 0 us
  local copies, waits for them, and re-layouts: 5.02 us -> 1.59 us
    psum x2 -> x0, waiting for transfers between devices: 113 us -> none  [the longest x1 69.2 us: layer_fn(): lax.psum((project(normed_mlp, w_gate), project(normed_mlp, w_up)), 'tx')]
    pallas_call x0 -> x1, Pallas kernels: none -> 72.9 us  [layer_fn(): pl.pallas_call(kernel, out_shape=jax.ShapeDtypeStruct((S, D1), bf16), in_...]
    dot_general x8 -> x0, matrix products: 43.1 us -> none  [the longest x7 41.3 us: project(): jnp.einsum('...c,ch->...h', rows_bf, weight, preferred_element_type=jnp.f...]
    reduce_scatter x2 -> x0, waiting for transfers between devices: 19.7 us -> none  [the longest x1 9.88 us: layer_fn(): lax.psum_scatter(project(act_val, w_down), 'ty', scatter_dimension=0, til...]
    psum x2 -> x0, blocking collectives: 15.1 us -> none  [norm_sharded(): moments = lax.psum(moments, 'tx')]
    all_gather x2 -> x0, blocking collectives: 12.2 us -> none  [the longest x1 6.17 us: layer_fn(): lax.all_gather(norm_sharded(resid_h, full_width), 'ty', axis=0, tiled=True)]
    convert_element_type x5 -> x0, other arithmetic: 4.17 us -> none  [the longest x1 1.62 us: layer_fn(): (resid_h.astype(jnp.float32) + mlp_out.astype(jnp.float32)).astype(jnp.bf...]
  transfers between devices with their start and end apart: 4 -> 0, of which waited for: 4 -> 0; matrix products, arithmetic and copies ran while one was open for 0% -> 0% of each run, Pallas kernels for 0% -> 0%
where the time goes in v1:
time: 74.6 us; the launch traced here: 74.5 us
  Pallas kernels  72.9 us (98%)
  local copies, waits for them, and re-layouts  1.59 us (2%)
    pallas_call x1, Pallas kernels, layer_fn(): pl.pallas_call(kernel, out_shape=jax.ShapeDtypeStruct((S, D1), bf16), in_...  72.9 us
    unnamed x1, local copies, waits for them, and re-layouts  1.59 us

profile of v1, /device:TPU:0, one launch (start us, length us, event | category | flops | bytes accessed | tf_op | source)
XLA Modules:
  0.0 74.5 jit_solution(2593401944293229390)
XLA Ops:
  0.0 72.9 %shard_map.100 = bf16[64,1280]{1,0:T(8,128)(2,1)} custom-call(bf16[64,1280]{1,0:T(8,128)(2,1)} %bitcast.3, bf16[1280,2560]{1,0:T(8,128)(2,1)} %wq.1, bf16[1280,2560]{1,0:T(8,128)(2,1)} %wk.1, bf16[1280,2560]{1,0:T(8,128)(2,1)} %wv.1, bf16[2560,1280]{1,0:T(8,128)(2,1)} %wo.1, bf16[1280,6912]{1,0:T(8,128)(2,1)} %wg.1, bf16[1280,6912]{1,0:T(8,128)(2,1)} %wu.1, ...), custom_call_target="tpu_custom_call" | custom-call | tf_op jit(solution)/shard_map/pallas_call | solution.py:440
  72.9 1.6 %copy.12 = bf16[1,64,1280]{2,1,0:T(8,128)(2,1)} copy(bf16[1,64,1280]{2,1,0:T(8,128)(2,1)} %bitcast.2) | data formatting | bytes 327680

commit v2 on v1

--- a/solution.py
+++ b/solution.py
@@ -94,11 +94,6 @@
             qkv_load(m, half).start()
     cos_load.start()
     sin_load.start()
-    for i in range(4):
-        wo_load(i).start()
-    for j in range(7):
-        gu_load(j, 0).start()
-        gu_load(j, 1).start()
 
     eye = lax.broadcasted_iota(jnp.int32, (S, 128), 0) == lax.broadcasted_iota(jnp.int32, (S, 128), 1)
     row8 = lax.broadcasted_iota(jnp.int32, (8, 128), 0)
@@ -140,19 +135,14 @@
     def q2_copy(r, m):
         return rcopy(XS.at[r, m], R2.at[r, m], q2_s.at[r, m], q2_r.at[r, m], xpeer)
 
-    def qkv_mm(r, m):
-        if r == 0:
-            qkv_load(m, 0).wait()
-            qkv_load(m, 1).wait()
-        n = NB[r]
-        for which in range(2):
-            half = co if which == 0 else c
-            dst = PS if which == 0 else PO
-            res = bdot(n, WB[pl.ds(pl.multiple_of((2 * m + half) * D1, D1), D1), :]).astype(bf16)
-            dst[r, m, 0] = res[:, :GW]
-            dst[r, m, 1] = res[:, GW:]
-            if which == 0:
-                q1_copy(r, m).start()
+    def qkv_mm(r, m, which):
+        half = co if which == 0 else c
+        dst = PS if which == 0 else PO
+        res = bdot(NB[r], WB[pl.ds(pl.multiple_of((2 * m + half) * D1, D1), D1), :]).astype(bf16)
+        dst[r, m, 0] = res[:, :GW]
+        dst[r, m, 1] = res[:, GW:]
+        if which == 0:
+            q1_copy(r, m).start()
 
     def qkv_s1(r, m):
         q1_copy(r, m).wait_recv()
@@ -162,24 +152,41 @@
     for k in range(1, 4):
         st1_copy(0, k).wait_recv()
     NB[0] = normalize(x_own, ST1[0, 0] + ST1[0, 1] + ST1[0, 2] + ST1[0, 3])
-    qkv_mm(0, 0)
-    qkv_mm(0, 1)
+    qkv_load(0, 0).wait()
+    qkv_load(0, 1).wait()
+    qkv_mm(0, 0, 0)
+    qkv_mm(0, 0, 1)
+    qkv_load(1, 0).wait()
+    qkv_load(1, 1).wait()
+    qkv_mm(0, 1, 0)
     qkv_s1(0, 0)
-    qkv_mm(0, 2)
+    qkv_mm(0, 1, 1)
+    qkv_load(2, 0).wait()
+    qkv_load(2, 1).wait()
+    for i in range(4):
+        wo_load(i).start()
+    for j in range(7):
+        gu_load(j, 0).start()
+        gu_load(j, 1).start()
+    qkv_mm(0, 2, 0)
     qkv_s1(0, 1)
+    qkv_mm(0, 2, 1)
 
     x_send.wait_recv()
     for k in range(4):
         st1_copy(1, k).wait_recv()
     NB[1] = normalize(XB[1].astype(f32), ST1[1, 0] + ST1[1, 1] + ST1[1, 2] + ST1[1, 3])
-    qkv_mm(1, 0)
+    qkv_mm(1, 0, 0)
     qkv_s1(0, 2)
-    qkv_mm(1, 1)
+    qkv_mm(1, 0, 1)
+    qkv_mm(1, 1, 0)
     qkv_s1(1, 0)
-    qkv_mm(1, 2)
+    qkv_mm(1, 1, 1)
+    qkv_mm(1, 2, 0)
+    qkv_s1(1, 1)
+    qkv_mm(1, 2, 1)
     for j in range(NJ):
         wd_load(j).start()
-    qkv_s1(1, 1)
     qkv_s1(1, 2)
 
     cos_load.wait()

time: 74.6 us -> 73.8 us (0.989)
  Pallas kernels: 72.9 us -> 72.1 us
    pallas_call x1, Pallas kernels: 72.9 us -> 72.1 us  [layer_fn(): pl.pallas_call(kernel, out_shape=jax.ShapeDtypeStruct((S, D1), bf16), in_...]
where the time goes in v2:
time: 73.8 us; the launch traced here: 73.7 us
  Pallas kernels  72.1 us (98%)
  local copies, waits for them, and re-layouts  1.59 us (2%)
    pallas_call x1, Pallas kernels, layer_fn(): pl.pallas_call(kernel, out_shape=jax.ShapeDtypeStruct((S, D1), bf16), in_...  72.1 us
    unnamed x1, local copies, waits for them, and re-layouts  1.59 us

profile of v2, /device:TPU:0, one launch (start us, length us, event | category | flops | bytes accessed | tf_op | source)
XLA Modules:
  0.0 73.7 jit_solution(9483851823528636908)
XLA Ops:
  0.0 72.1 %shard_map.100 = bf16[64,1280]{1,0:T(8,128)(2,1)} custom-call(bf16[64,1280]{1,0:T(8,128)(2,1)} %bitcast.3, bf16[1280,2560]{1,0:T(8,128)(2,1)} %wq.1, bf16[1280,2560]{1,0:T(8,128)(2,1)} %wk.1, bf16[1280,2560]{1,0:T(8,128)(2,1)} %wv.1, bf16[2560,1280]{1,0:T(8,128)(2,1)} %wo.1, bf16[1280,6912]{1,0:T(8,128)(2,1)} %wg.1, bf16[1280,6912]{1,0:T(8,128)(2,1)} %wu.1, ...), custom_call_target="tpu_custom_call" | custom-call | tf_op jit(solution)/shard_map/pallas_call | solution.py:447
  72.1 1.6 %copy.12 = bf16[1,64,1280]{2,1,0:T(8,128)(2,1)} copy(bf16[1,64,1280]{2,1,0:T(8,128)(2,1)} %bitcast.2) | data formatting | bytes 327680

commit v3 on v2

--- a/solution.py
+++ b/solution.py
@@ -21,8 +21,8 @@
 CH = 768
 NJ = 9
 NU = 2 * NJ
-NP = 4
-L1, L2, L3, L4 = 1, 3, 5, 6
+NP = 5
+L1, L2, L3, L4 = 1, 4, 7, 8
 
 
 def rotary_tables():
@@ -41,7 +41,7 @@
 def kernel(
     x_hbm, wq, wk, wv, wo, wg, wu, wd, cos_hbm, sin_hbm, y_hbm,
     WA, WB, XB, NB, HB, ST1, ST2, PS, PO, R1, XS, R2, OF, AO, AR,
-    MP, MR1, MXS, MR2, AF, ACC, DS, DR, COS, SIN, YB,
+    MP, MR1, MXS, MR2, AF, ACC, DS, DR, COS, SIN,
     wsem, lsem, xg_s, xg_r, st1_s, st1_r, st2_s, st2_r,
     q1_s, q1_r, q2_s, q2_r, ox_s, ox_r, od_s, od_r, ay_s, ay_r,
     m1_s, m1_r, m2_s, m2_r, ax_s, ax_r, ad_s, ad_r, dy_s, dy_r,
@@ -130,23 +130,35 @@
         st1_copy(1, k).start()
 
     def q1_copy(r, m):
-        return rcopy(PS.at[r, m], R1.at[r, m], q1_s.at[r, m], q1_r.at[r, m], partner)
+        return rcopy(PS.at[m], R1.at[r, m], q1_s.at[r, m], q1_r.at[r, m], partner)
 
     def q2_copy(r, m):
-        return rcopy(XS.at[r, m], R2.at[r, m], q2_s.at[r, m], q2_r.at[r, m], xpeer)
-
-    def qkv_mm(r, m, which):
-        half = co if which == 0 else c
-        dst = PS if which == 0 else PO
-        res = bdot(NB[r], WB[pl.ds(pl.multiple_of((2 * m + half) * D1, D1), D1), :]).astype(bf16)
-        dst[r, m, 0] = res[:, :GW]
-        dst[r, m, 1] = res[:, GW:]
-        if which == 0:
-            q1_copy(r, m).start()
+        return rcopy(XS.at[m], R2.at[r, m], q2_s.at[r, m], q2_r.at[r, m], xpeer)
+
+    def qkv_dot(r, m, half):
+        return bdot(NB[r], WB[pl.ds(pl.multiple_of((2 * m + half) * D1, D1), D1), :]).astype(bf16)
+
+    def put_send(r, m, res):
+        if r == 1:
+            q1_copy(0, m).wait_send()
+        PS[m, 0] = res[:, :GW]
+        PS[m, 1] = res[:, GW:]
+        q1_copy(r, m).start()
+
+    def put_keep(r, m, res):
+        PO[r, m, 0] = res[:, :GW]
+        PO[r, m, 1] = res[:, GW:]
+
+    def qkv_mm(r, m):
+        sent, kept = qkv_dot(r, m, co), qkv_dot(r, m, c)
+        put_send(r, m, sent)
+        put_keep(r, m, kept)
 
     def qkv_s1(r, m):
         q1_copy(r, m).wait_recv()
-        XS[r, m] = (PO[r, m, xo].astype(f32) + R1[r, m, xo].astype(f32)).astype(bf16)
+        if r == 1:
+            q2_copy(0, m).wait_send()
+        XS[m] = (PO[r, m, xo].astype(f32) + R1[r, m, xo].astype(f32)).astype(bf16)
         q2_copy(r, m).start()
 
     for k in range(1, 4):
@@ -154,13 +166,12 @@
     NB[0] = normalize(x_own, ST1[0, 0] + ST1[0, 1] + ST1[0, 2] + ST1[0, 3])
     qkv_load(0, 0).wait()
     qkv_load(0, 1).wait()
-    qkv_mm(0, 0, 0)
-    qkv_mm(0, 0, 1)
+    put_send(0, 0, qkv_dot(0, 0, co))
+    put_keep(0, 0, qkv_dot(0, 0, c))
     qkv_load(1, 0).wait()
     qkv_load(1, 1).wait()
-    qkv_mm(0, 1, 0)
     qkv_s1(0, 0)
-    qkv_mm(0, 1, 1)
+    qkv_mm(0, 1)
     qkv_load(2, 0).wait()
     qkv_load(2, 1).wait()
     for i in range(4):
@@ -168,26 +179,21 @@
     for j in range(7):
         gu_load(j, 0).start()
         gu_load(j, 1).start()
-    qkv_mm(0, 2, 0)
+    qkv_mm(0, 2)
     qkv_s1(0, 1)
-    qkv_mm(0, 2, 1)
 
     x_send.wait_recv()
     for k in range(4):
         st1_copy(1, k).wait_recv()
     NB[1] = normalize(XB[1].astype(f32), ST1[1, 0] + ST1[1, 1] + ST1[1, 2] + ST1[1, 3])
-    qkv_mm(1, 0, 0)
+    qkv_mm(1, 0)
     qkv_s1(0, 2)
-    qkv_mm(1, 0, 1)
-    qkv_mm(1, 1, 0)
+    qkv_mm(1, 1)
     qkv_s1(1, 0)
-    qkv_mm(1, 1, 1)
-    qkv_mm(1, 2, 0)
-    qkv_s1(1, 1)
-    qkv_mm(1, 2, 1)
+    qkv_mm(1, 2)
     for j in range(NJ):
         wd_load(j).start()
-    qkv_s1(1, 2)
+    qkv_s1(1, 1)
 
     cos_load.wait()
     sin_load.wait()
@@ -235,21 +241,28 @@
     def ay_copy(r):
         return rcopy(AO.at[r], AR.at[1 - r], ay_s.at[r], ay_r.at[1 - r], ypeer)
 
+    def out_half(r, half):
+        o = jnp.concatenate([OF[r, half, 0], OF[r, half, 1]], axis=1)
+        return bdot(o, WA[14 + half]), bdot(o, WA[16 + half, :, : D1 - CH])
+
     def out_proj(r):
         if r == 0:
             for i in range(4):
                 wo_load(i).wait()
+        lo, hi = out_half(r, c)
+        ACC[:, :CH] = lo
+        ACC[:, CH:] = hi
         od_recv(r).wait_recv()
-        o0 = jnp.concatenate([OF[r, 0, 0], OF[r, 0, 1]], axis=1)
-        o1 = jnp.concatenate([OF[r, 1, 0], OF[r, 1, 1]], axis=1)
-        AO[r, :, :CH] = (bdot(o0, WA[14]) + bdot(o1, WA[15])).astype(bf16)
-        AO[r, :, CH:] = (bdot(o0, WA[16, :, : D1 - CH]) + bdot(o1, WA[17, :, : D1 - CH])).astype(bf16)
+        lo, hi = out_half(r, co)
+        AO[r, :, :CH] = (ACC[:, :CH] + lo).astype(bf16)
+        AO[r, :, CH:] = (ACC[:, CH:] + hi).astype(bf16)
         ay_copy(r).start()
 
     attention(0)
-    attention(1)
+    qkv_s1(1, 2)
     o_forward(0)
     out_proj(0)
+    attention(1)
     o_forward(1)
     out_proj(1)
     for j in range(7, NJ):
@@ -385,8 +398,9 @@
 
     dy_copy().wait_recv()
     mlp = (ACC[...] + DR[...].astype(f32)).astype(bf16)
-    YB[...] = (HB[0].astype(f32) + mlp.astype(f32)).astype(bf16)
-    y_store = pltpu.make_async_copy(YB, y_hbm, lsem.at[0])
+    ay_copy(0).wait_send()
+    AO[0] = (HB[0].astype(f32) + mlp.astype(f32)).astype(bf16)
+    y_store = pltpu.make_async_copy(AO.at[0], y_hbm, lsem.at[0])
     y_store.start()
     for k in range(1, 4):
         st1_copy(0, k).wait_send()
@@ -395,11 +409,13 @@
     x_send.wait_send()
     for r in range(2):
         for m in range(3):
-            q1_copy(r, m).wait_send()
-            q2_copy(r, m).wait_send()
+            if r == 1:
+                q1_copy(r, m).wait_send()
+                q2_copy(r, m).wait_send()
         ox_copy(r).wait_send()
         od_copy(r).wait_send()
-        ay_copy(r).wait_send()
+        if r == 1:
+            ay_copy(r).wait_send()
         for k in range(1, 4):
             st2_copy(r, k).wait_send()
     dy_copy().wait_send()
@@ -418,10 +434,10 @@
         vm((2, S, D1), bf16),
         vm((2, 4, 8, 128), f32),
         vm((2, 4, 8, 128), f32),
+        vm((3, 2, S, GW), bf16),
         vm((2, 3, 2, S, GW), bf16),
         vm((2, 3, 2, S, GW), bf16),
-        vm((2, 3, 2, S, GW), bf16),
-        vm((2, 3, S, GW), bf16),
+        vm((3, S, GW), bf16),
         vm((2, 3, S, GW), bf16),
         vm((2, 2, 2, S, GW), bf16),
         vm((2, S, D1), bf16),
@@ -436,7 +452,6 @@
         vm((S, D1), bf16),
         vm((S, HEAD_DIM), f32),
         vm((S, HEAD_DIM), f32),
-        vm((S, D1), bf16),
         dma((37,)), dma((3,)), dma((1,)), dma((1,)),
         dma((2, 4)), dma((2, 4)), dma((2, 4)), dma((2, 4)),
         dma((2, 3)), dma((2, 3)), dma((2, 3)), dma((2, 3)),

time: 73.8 us -> 74 us (level)
  no operation moved by 1% of the time
where the time goes in v3:
time: 74 us; the launch traced here: 73.9 us
  Pallas kernels  72.3 us (98%)
  local copies, waits for them, and re-layouts  1.59 us (2%)
    pallas_call x1, Pallas kernels, layer_fn(): pl.pallas_call(kernel, out_shape=jax.ShapeDtypeStruct((S, D1), bf16), in_...  72.3 us
    unnamed x1, local copies, waits for them, and re-layouts  1.59 us

profile of v3, /device:TPU:0, one launch (start us, length us, event | category | flops | bytes accessed | tf_op | source)
XLA Modules:
  0.0 73.9 jit_solution(8440306033828608820)
XLA Ops:
  0.0 72.3 %shard_map.100 = bf16[64,1280]{1,0:T(8,128)(2,1)} custom-call(bf16[64,1280]{1,0:T(8,128)(2,1)} %bitcast.3, bf16[1280,2560]{1,0:T(8,128)(2,1)} %wq.1, bf16[1280,2560]{1,0:T(8,128)(2,1)} %wk.1, bf16[1280,2560]{1,0:T(8,128)(2,1)} %wv.1, bf16[2560,1280]{1,0:T(8,128)(2,1)} %wo.1, bf16[1280,6912]{1,0:T(8,128)(2,1)} %wg.1, bf16[1280,6912]{1,0:T(8,128)(2,1)} %wu.1, ...), custom_call_target="tpu_custom_call" | custom-call | tf_op jit(solution)/shard_map/pallas_call | solution.py:462
  72.3 1.6 %copy.12 = bf16[1,64,1280]{2,1,0:T(8,128)(2,1)} copy(bf16[1,64,1280]{2,1,0:T(8,128)(2,1)} %bitcast.2) | data formatting | bytes 327680

commit v4 on v3

--- a/solution.py
+++ b/solution.py
@@ -22,6 +22,7 @@
 NJ = 9
 NU = 2 * NJ
 NP = 5
+PARTS = ((0, 384), (384, 256))
 L1, L2, L3, L4 = 1, 4, 7, 8
 
 
@@ -41,7 +42,7 @@
 def kernel(
     x_hbm, wq, wk, wv, wo, wg, wu, wd, cos_hbm, sin_hbm, y_hbm,
     WA, WB, XB, NB, HB, ST1, ST2, PS, PO, R1, XS, R2, OF, AO, AR,
-    MP, MR1, MXS, MR2, AF, ACC, DS, DR, COS, SIN,
+    MP, MR1, MXS, MR2, AF, ACC, DS, DR, COS, SIN, PR,
     wsem, lsem, xg_s, xg_r, st1_s, st1_r, st2_s, st2_r,
     q1_s, q1_r, q2_s, q2_r, ox_s, ox_r, od_s, od_r, ay_s, ay_r,
     m1_s, m1_r, m2_s, m2_r, ax_s, ax_r, ad_s, ad_r, dy_s, dy_r,
@@ -132,8 +133,9 @@
     def q1_copy(r, m):
         return rcopy(PS.at[m], R1.at[r, m], q1_s.at[r, m], q1_r.at[r, m], partner)
 
-    def q2_copy(r, m):
-        return rcopy(XS.at[m], R2.at[r, m], q2_s.at[r, m], q2_r.at[r, m], xpeer)
+    def q2_copy(r, m, p=0):
+        lanes = pl.ds(*(PARTS[p] if r == 1 and m == 2 else (0, GW)))
+        return rcopy(XS.at[m, :, lanes], R2.at[r, m, :, lanes], q2_s.at[r, m + p], q2_r.at[r, m + p], xpeer)
 
     def qkv_dot(r, m, half):
         return bdot(NB[r], WB[pl.ds(pl.multiple_of((2 * m + half) * D1, D1), D1), :]).astype(bf16)
@@ -150,6 +152,13 @@
         PO[r, m, 1] = res[:, GW:]
 
     def qkv_mm(r, m):
+        if r == 0:
+            qkv_load(m, 0).wait()
+            qkv_load(m, 1).wait()
+        put_send(r, m, qkv_dot(r, m, co))
+        put_keep(r, m, qkv_dot(r, m, c))
+
+    def qkv_mm_both(r, m):
         sent, kept = qkv_dot(r, m, co), qkv_dot(r, m, c)
         put_send(r, m, sent)
         put_keep(r, m, kept)
@@ -160,83 +169,62 @@
             q2_copy(0, m).wait_send()
         XS[m] = (PO[r, m, xo].astype(f32) + R1[r, m, xo].astype(f32)).astype(bf16)
         q2_copy(r, m).start()
-
-    for k in range(1, 4):
-        st1_copy(0, k).wait_recv()
-    NB[0] = normalize(x_own, ST1[0, 0] + ST1[0, 1] + ST1[0, 2] + ST1[0, 3])
-    qkv_load(0, 0).wait()
-    qkv_load(0, 1).wait()
-    put_send(0, 0, qkv_dot(0, 0, co))
-    put_keep(0, 0, qkv_dot(0, 0, c))
-    qkv_load(1, 0).wait()
-    qkv_load(1, 1).wait()
-    qkv_s1(0, 0)
-    qkv_mm(0, 1)
-    qkv_load(2, 0).wait()
-    qkv_load(2, 1).wait()
-    for i in range(4):
-        wo_load(i).start()
-    for j in range(7):
-        gu_load(j, 0).start()
-        gu_load(j, 1).start()
-    qkv_mm(0, 2)
-    qkv_s1(0, 1)
-
-    x_send.wait_recv()
-    for k in range(4):
-        st1_copy(1, k).wait_recv()
-    NB[1] = normalize(XB[1].astype(f32), ST1[1, 0] + ST1[1, 1] + ST1[1, 2] + ST1[1, 3])
-    qkv_mm(1, 0)
-    qkv_s1(0, 2)
-    qkv_mm(1, 1)
-    qkv_s1(1, 0)
-    qkv_mm(1, 2)
-    for j in range(NJ):
-        wd_load(j).start()
-    qkv_s1(1, 1)
+        if r == 1 and m == 2:
+            q2_copy(r, m, 1).start()
 
     cos_load.wait()
     sin_load.wait()
     causal = lax.broadcasted_iota(jnp.int32, (S, S), 0) >= lax.broadcasted_iota(jnp.int32, (S, S), 1)
 
-    def ox_copy(r):
-        return rcopy(OF.at[r, c, xx], OF.at[r, c, xx], ox_s.at[r], ox_r.at[r], xpeer)
-
-    def ox_recv(r):
-        return rcopy(OF.at[r, c, xo], OF.at[r, c, xo], ox_s.at[r], ox_r.at[r], xpeer)
-
-    def od_copy(r):
-        return rcopy(OF.at[r, c], OF.at[r, c], od_s.at[r], od_r.at[r], partner)
-
-    def od_recv(r):
-        return rcopy(OF.at[r, co], OF.at[r, co], od_s.at[r], od_r.at[r], partner)
-
-    def attention(r):
+    def o_lanes(r, p):
+        return pl.ds(*(PARTS[p] if r == 1 else (0, GW)))
+
+    def ox_copy(r, p=0):
+        ref = OF.at[r, c, xx, :, o_lanes(r, p)]
+        return rcopy(ref, ref, ox_s.at[r + p], ox_r.at[r + p], xpeer)
+
+    def ox_recv(r, p=0):
+        ref = OF.at[r, c, xo, :, o_lanes(r, p)]
+        return rcopy(ref, ref, ox_s.at[r + p], ox_r.at[r + p], xpeer)
+
+    def od_copy(r, p=0):
+        ref = OF.at[r, c, :, :, o_lanes(r, p)]
+        return rcopy(ref, ref, od_s.at[r + p], od_r.at[r + p], partner)
+
+    def od_recv(r, p=0):
+        ref = OF.at[r, co, :, :, o_lanes(r, p)]
+        return rcopy(ref, ref, od_s.at[r + p], od_r.at[r + p], partner)
+
+    def total(r, m, lanes):
+        return (PO[r, m, xx, :, lanes].astype(f32) + R1[r, m, xx, :, lanes].astype(f32) + R2[r, m, :, lanes].astype(f32)).astype(bf16)
+
+    def scores(r):
         cos_t, sin_t = COS[...], SIN[...]
-        full = []
-        for m in range(3):
-            q2_copy(r, m).wait_recv()
-            full.append((PO[r, m, xx].astype(f32) + R1[r, m, xx].astype(f32) + R2[r, m].astype(f32)).astype(bf16))
-
-        def rot(v):
-            v = v.astype(f32)
+        q2_copy(r, 0).wait_recv()
+        q2_copy(r, 1).wait_recv()
+
+        def rot(m, h):
+            v = total(r, m, pl.ds(h * HEAD_DIM, HEAD_DIM)).astype(f32)
             return (v * cos_t + pltpu.roll(v, HEAD_DIM // 2, 1) * sin_t).astype(bf16)
 
-        outs = []
+        qs, ks = [rot(0, h) for h in range(GH)], [rot(1, h) for h in range(GH)]
+        sc = [lax.dot_general(q, k, (((1,), (1,)), ((), ())), preferred_element_type=f32) * HEAD_DIM ** -0.5 for q, k in zip(qs, ks)]
+        sc = [jnp.where(causal, v, -1e30) for v in sc]
+        ex = [jnp.exp(v - jnp.max(v, axis=1, keepdims=True)) for v in sc]
         for h in range(GH):
-            cols = slice(h * HEAD_DIM, (h + 1) * HEAD_DIM)
-            qh, kh, vh = rot(full[0][:, cols]), rot(full[1][:, cols]), full[2][:, cols]
-            sc = lax.dot_general(qh, kh, (((1,), (1,)), ((), ())), preferred_element_type=f32) * HEAD_DIM ** -0.5
-            sc = jnp.where(causal, sc, -1e30)
-            e = jnp.exp(sc - jnp.max(sc, axis=1, keepdims=True))
-            p = (e / jnp.sum(e, axis=1, keepdims=True)).astype(bf16)
-            outs.append(bdot(p, vh).astype(bf16))
-        OF[r, c, xx] = jnp.concatenate(outs, axis=1)
-        ox_copy(r).start()
-
-    def o_forward(r):
-        ox_recv(r).wait_recv()
-        od_copy(r).start()
+            PR[h] = (ex[h] / jnp.sum(ex[h], axis=1, keepdims=True)).astype(bf16)
+
+    def values(r, p=0):
+        q2_copy(r, 2, p).wait_recv()
+        off, size = PARTS[p] if r == 1 else (0, GW)
+        heads = range(off // HEAD_DIM, (off + size) // HEAD_DIM)
+        outs = [bdot(PR[h], total(r, 2, pl.ds(h * HEAD_DIM, HEAD_DIM))).astype(bf16) for h in heads]
+        OF[r, c, xx, :, off:off + size] = jnp.concatenate(outs, axis=1)
+        ox_copy(r, p).start()
+
+    def o_forward(r, p=0):
+        ox_recv(r, p).wait_recv()
+        od_copy(r, p).start()
 
     def ay_copy(r):
         return rcopy(AO.at[r], AR.at[1 - r], ay_s.at[r], ay_r.at[1 - r], ypeer)
@@ -253,17 +241,48 @@
         ACC[:, :CH] = lo
         ACC[:, CH:] = hi
         od_recv(r).wait_recv()
+        if r == 1:
+            od_recv(r, 1).wait_recv()
         lo, hi = out_half(r, co)
         AO[r, :, :CH] = (ACC[:, :CH] + lo).astype(bf16)
         AO[r, :, CH:] = (ACC[:, CH:] + hi).astype(bf16)
         ay_copy(r).start()
 
-    attention(0)
+    for k in range(1, 4):
+        st1_copy(0, k).wait_recv()
+    NB[0] = normalize(x_own, ST1[0, 0] + ST1[0, 1] + ST1[0, 2] + ST1[0, 3])
+    qkv_mm(0, 0)
+    qkv_s1(0, 0)
+    qkv_mm(0, 1)
+    qkv_s1(0, 1)
+    qkv_mm(0, 2)
+    for i in range(4):
+        wo_load(i).start()
+    for j in range(7):
+        gu_load(j, 0).start()
+        gu_load(j, 1).start()
+    x_send.wait_recv()
+    for k in range(4):
+        st1_copy(1, k).wait_recv()
+    NB[1] = normalize(XB[1].astype(f32), ST1[1, 0] + ST1[1, 1] + ST1[1, 2] + ST1[1, 3])
+    qkv_s1(0, 2)
+    qkv_mm(1, 0)
+    qkv_s1(1, 0)
+    scores(0)
+    qkv_mm_both(1, 1)
+    values(0)
+    qkv_s1(1, 1)
+    qkv_mm_both(1, 2)
+    for j in range(NJ):
+        wd_load(j).start()
     qkv_s1(1, 2)
     o_forward(0)
     out_proj(0)
-    attention(1)
-    o_forward(1)
+    scores(1)
+    values(1, 0)
+    values(1, 1)
+    o_forward(1, 0)
+    o_forward(1, 1)
     out_proj(1)
     for j in range(7, NJ):
         gu_load(j, 0).start()
@@ -412,8 +431,11 @@
             if r == 1:
                 q1_copy(r, m).wait_send()
                 q2_copy(r, m).wait_send()
-        ox_copy(r).wait_send()
-        od_copy(r).wait_send()
+        if r == 1:
+            q2_copy(1, 2, 1).wait_send()
+        for p in range(r + 1):
+            ox_copy(r, p).wait_send()
+            od_copy(r, p).wait_send()
         if r == 1:
             ay_copy(r).wait_send()
         for k in range(1, 4):
@@ -452,10 +474,11 @@
         vm((S, D1), bf16),
         vm((S, HEAD_DIM), f32),
         vm((S, HEAD_DIM), f32),
+        vm((GH, S, S), bf16),
         dma((37,)), dma((3,)), dma((1,)), dma((1,)),
         dma((2, 4)), dma((2, 4)), dma((2, 4)), dma((2, 4)),
-        dma((2, 3)), dma((2, 3)), dma((2, 3)), dma((2, 3)),
-        dma((2,)), dma((2,)), dma((2,)), dma((2,)), dma((2,)), dma((2,)),
+        dma((2, 3)), dma((2, 3)), dma((2, 4)), dma((2, 4)),
+        dma((3,)), dma((3,)), dma((3,)), dma((3,)), dma((2,)), dma((2,)),
         dma((NJ,)), dma((NJ,)), dma((NJ,)), dma((NJ,)),
         dma((NJ,)), dma((NJ,)), dma((NJ,)), dma((NJ,)), dma((1,)), dma((1,)),
     ]

time: 74 us -> 73.1 us (0.988)
  Pallas kernels: 72.3 us -> 71.4 us
    pallas_call x1, Pallas kernels: 72.3 us -> 71.4 us  [layer_fn(): pl.pallas_call(kernel, out_shape=jax.ShapeDtypeStruct((S, D1), bf16), in_...]
where the time goes in v4:
time: 73.1 us; the launch traced here: 73 us
  Pallas kernels  71.4 us (98%)
  local copies, waits for them, and re-layouts  1.59 us (2%)
    pallas_call x1, Pallas kernels, layer_fn(): pl.pallas_call(kernel, out_shape=jax.ShapeDtypeStruct((S, D1), bf16), in_...  71.4 us
    unnamed x1, local copies, waits for them, and re-layouts  1.59 us

profile of v4, /device:TPU:0, one launch (start us, length us, event | category | flops | bytes accessed | tf_op | source)
XLA Modules:
  0.0 73.0 jit_solution(5983945331430992160)
XLA Ops:
  0.0 71.4 %shard_map.100 = bf16[64,1280]{1,0:T(8,128)(2,1)} custom-call(bf16[64,1280]{1,0:T(8,128)(2,1)} %bitcast.3, bf16[1280,2560]{1,0:T(8,128)(2,1)} %wq.1, bf16[1280,2560]{1,0:T(8,128)(2,1)} %wk.1, bf16[1280,2560]{1,0:T(8,128)(2,1)} %wv.1, bf16[2560,1280]{1,0:T(8,128)(2,1)} %wo.1, bf16[1280,6912]{1,0:T(8,128)(2,1)} %wg.1, bf16[1280,6912]{1,0:T(8,128)(2,1)} %wu.1, ...), custom_call_target="tpu_custom_call" | custom-call | tf_op jit(solution)/shard_map/pallas_call | solution.py:485
  71.4 1.6 %copy.12 = bf16[1,64,1280]{2,1,0:T(8,128)(2,1)} copy(bf16[1,64,1280]{2,1,0:T(8,128)(2,1)} %bitcast.2) | data formatting | bytes 327680

commit v5 on v4

--- a/solution.py
+++ b/solution.py
@@ -23,7 +23,7 @@
 NU = 2 * NJ
 NP = 5
 PARTS = ((0, 384), (384, 256))
-L1, L2, L3, L4 = 1, 4, 7, 8
+L1, L2, L3, L4 = 1, 4, 7, 9
 
 
 def rotary_tables():
@@ -74,21 +74,23 @@
 
     def qkv_load(m, half):
         src = (wq, wk, wv)[m].at[:, pl.ds(half * D1, D1)]
-        return pltpu.make_async_copy(src, WB.at[pl.ds((2 * m + half) * D1, D1), :], wsem.at[2 * m + half])
+        return pltpu.make_async_copy(src, WB.at[pl.ds((2 * m + half) * D1, D1), :], wsem.at[m])
 
     def wo_load(i):
         kh, wide = i % 2, i // 2
         if wide == 0:
-            return pltpu.make_async_copy(wo.at[pl.ds(kh * D1, D1), pl.ds(0, CH)], WA.at[14 + i], wsem.at[6 + i])
-        return pltpu.make_async_copy(wo.at[pl.ds(kh * D1, D1), pl.ds(CH, D1 - CH)], WA.at[14 + i, :, pl.ds(0, D1 - CH)], wsem.at[6 + i])
+            return pltpu.make_async_copy(wo.at[pl.ds(kh * D1, D1), pl.ds(0, CH)], WA.at[14 + i], wsem.at[3])
+        return pltpu.make_async_copy(wo.at[pl.ds(kh * D1, D1), pl.ds(CH, D1 - CH)], WA.at[14 + i, :, pl.ds(0, D1 - CH)], wsem.at[4])
 
     def gu_load(j, which):
-        off = pl.multiple_of(j * CH, CH)
-        return pltpu.make_async_copy((wg, wu)[which].at[:, pl.ds(off, CH)], WA.at[2 * j + which], wsem.at[10 + 2 * j + which])
-
-    def wd_load(j):
-        off = pl.multiple_of(j * CH, CH)
-        return pltpu.make_async_copy(wd.at[pl.ds(off, CH), :], WB.at[pl.ds(off, CH), :], wsem.at[28 + j])
+        group = 5 if j < 2 else 6 if j < 7 else 7
+        return pltpu.make_async_copy((wg, wu)[which].at[:, pl.ds(j * CH, CH)], WA.at[2 * j + which], wsem.at[group])
+
+    def wd_load():
+        return pltpu.make_async_copy(wd, WB.at[pl.ds(0, NJ * CH), :], wsem.at[8])
+
+    def await_all(ref, sem):
+        pltpu.make_async_copy(ref, ref, wsem.at[sem]).wait()
 
     for m in range(3):
         for half in range(2):
@@ -116,12 +118,16 @@
 
     x_load.wait()
     x_own = XB[0].astype(f32)
-    ST1[0, 0] = stats_tile(x_own)
+    ST1[0] = stats_tile(x_own)
     pl.semaphore_wait(barrier, 7)
 
     def st1_copy(r, k):
         dev = {"tx": lax.rem(tx + k, 4)} if r == 0 else {"ty": tyo, "tx": lax.rem(tx + k, 4)}
-        return rcopy(ST1.at[0, 0], ST1.at[r, k], st1_s.at[r, k], st1_r.at[r, k], dev)
+        return rcopy(ST1.at[0], ST1.at[4 * r + k], st1_s.at[0], st1_r.at[r], dev)
+
+    def st1_all(first, count, r):
+        ref = ST1.at[pl.ds(first, count)]
+        return rcopy(ref, ref, st1_s.at[0], st1_r.at[r], partner)
 
     for k in range(1, 4):
         st1_copy(0, k).start()
@@ -131,11 +137,11 @@
         st1_copy(1, k).start()
 
     def q1_copy(r, m):
-        return rcopy(PS.at[m], R1.at[r, m], q1_s.at[r, m], q1_r.at[r, m], partner)
+        return rcopy(PS.at[m], R1.at[r, m], q1_s.at[m], q1_r.at[r, m], partner)
 
     def q2_copy(r, m, p=0):
         lanes = pl.ds(*(PARTS[p] if r == 1 and m == 2 else (0, GW)))
-        return rcopy(XS.at[m, :, lanes], R2.at[r, m, :, lanes], q2_s.at[r, m + p], q2_r.at[r, m + p], xpeer)
+        return rcopy(XS.at[m, :, lanes], R2.at[r, m, :, lanes], q2_s.at[m + p], q2_r.at[3 * r + m + p], xpeer)
 
     def qkv_dot(r, m, half):
         return bdot(NB[r], WB[pl.ds(pl.multiple_of((2 * m + half) * D1, D1), D1), :]).astype(bf16)
@@ -153,8 +159,7 @@
 
     def qkv_mm(r, m):
         if r == 0:
-            qkv_load(m, 0).wait()
-            qkv_load(m, 1).wait()
+            await_all(WB.at[pl.ds(2 * m * D1, 2 * D1), :], m)
         put_send(r, m, qkv_dot(r, m, co))
         put_keep(r, m, qkv_dot(r, m, c))
 
@@ -172,8 +177,6 @@
         if r == 1 and m == 2:
             q2_copy(r, m, 1).start()
 
-    cos_load.wait()
-    sin_load.wait()
     causal = lax.broadcasted_iota(jnp.int32, (S, S), 0) >= lax.broadcasted_iota(jnp.int32, (S, S), 1)
 
     def o_lanes(r, p):
@@ -199,6 +202,9 @@
         return (PO[r, m, xx, :, lanes].astype(f32) + R1[r, m, xx, :, lanes].astype(f32) + R2[r, m, :, lanes].astype(f32)).astype(bf16)
 
     def scores(r):
+        if r == 0:
+            cos_load.wait()
+            sin_load.wait()
         cos_t, sin_t = COS[...], SIN[...]
         q2_copy(r, 0).wait_recv()
         q2_copy(r, 1).wait_recv()
@@ -233,13 +239,15 @@
         o = jnp.concatenate([OF[r, half, 0], OF[r, half, 1]], axis=1)
         return bdot(o, WA[14 + half]), bdot(o, WA[16 + half, :, : D1 - CH])
 
-    def out_proj(r):
+    def out_own(r):
         if r == 0:
-            for i in range(4):
-                wo_load(i).wait()
+            await_all(WA.at[pl.ds(14, 2)], 3)
+            await_all(WA.at[pl.ds(16, 2), :, pl.ds(0, D1 - CH)], 4)
         lo, hi = out_half(r, c)
         ACC[:, :CH] = lo
         ACC[:, CH:] = hi
+
+    def out_rest(r):
         od_recv(r).wait_recv()
         if r == 1:
             od_recv(r, 1).wait_recv()
@@ -248,9 +256,8 @@
         AO[r, :, CH:] = (ACC[:, CH:] + hi).astype(bf16)
         ay_copy(r).start()
 
-    for k in range(1, 4):
-        st1_copy(0, k).wait_recv()
-    NB[0] = normalize(x_own, ST1[0, 0] + ST1[0, 1] + ST1[0, 2] + ST1[0, 3])
+    st1_all(1, 3, 0).wait_recv()
+    NB[0] = normalize(x_own, ST1[0] + ST1[1] + ST1[2] + ST1[3])
     qkv_mm(0, 0)
     qkv_s1(0, 0)
     qkv_mm(0, 1)
@@ -262,9 +269,8 @@
         gu_load(j, 0).start()
         gu_load(j, 1).start()
     x_send.wait_recv()
-    for k in range(4):
-        st1_copy(1, k).wait_recv()
-    NB[1] = normalize(XB[1].astype(f32), ST1[1, 0] + ST1[1, 1] + ST1[1, 2] + ST1[1, 3])
+    st1_all(4, 4, 1).wait_recv()
+    NB[1] = normalize(XB[1].astype(f32), ST1[4] + ST1[5] + ST1[6] + ST1[7])
     qkv_s1(0, 2)
     qkv_mm(1, 0)
     qkv_s1(1, 0)
@@ -273,23 +279,28 @@
     values(0)
     qkv_s1(1, 1)
     qkv_mm_both(1, 2)
-    for j in range(NJ):
-        wd_load(j).start()
+    wd_load().start()
     qkv_s1(1, 2)
     o_forward(0)
-    out_proj(0)
+    out_own(0)
     scores(1)
+    out_rest(0)
     values(1, 0)
     values(1, 1)
     o_forward(1, 0)
     o_forward(1, 1)
-    out_proj(1)
+    out_own(1)
+    out_rest(1)
     for j in range(7, NJ):
         gu_load(j, 0).start()
         gu_load(j, 1).start()
 
     def st2_copy(r, k):
-        return rcopy(ST2.at[r, 0], ST2.at[r, k], st2_s.at[r, k], st2_r.at[r, k], {"tx": lax.rem(tx + k, 4)})
+        return rcopy(ST2.at[r, 0], ST2.at[r, k], st2_s.at[r], st2_r.at[r], {"tx": lax.rem(tx + k, 4)})
+
+    def st2_all(r):
+        ref = ST2.at[r, pl.ds(1, 3)]
+        return rcopy(ref, ref, st2_s.at[r], st2_r.at[r], partner)
 
     def residual(r):
         ay_copy(1 - r).wait_recv()
@@ -301,30 +312,29 @@
             st2_copy(r, k).start()
 
     def norm2(r):
-        for k in range(1, 4):
-            st2_copy(r, k).wait_recv()
+        st2_all(r).wait_recv()
         NB[r] = normalize(HB[r].astype(f32), ST2[r, 0] + ST2[r, 1] + ST2[r, 2] + ST2[r, 3])
 
     residual(1)
     norm2(1)
 
     def m1_copy(u, j):
-        return rcopy(MP.at[lax.rem(u, NP), pl.ds(2 * co, 2)], MR1.at[j], m1_s.at[j], m1_r.at[j], partner)
-
-    def m2_copy(j):
-        return rcopy(MXS.at[j], MR2.at[j], m2_s.at[j], m2_r.at[j], xpeer)
-
-    def ax_copy(j):
-        return rcopy(AF.at[j, 2 * c + xx], AF.at[j, 2 * c + xx], ax_s.at[j], ax_r.at[j], xpeer)
-
-    def ax_recv(j):
-        return rcopy(AF.at[j, 2 * c + xo], AF.at[j, 2 * c + xo], ax_s.at[j], ax_r.at[j], xpeer)
-
-    def ad_copy(j):
-        return rcopy(AF.at[j, pl.ds(2 * c, 2)], AF.at[j, pl.ds(2 * c, 2)], ad_s.at[j], ad_r.at[j], partner)
-
-    def ad_recv(j):
-        return rcopy(AF.at[j, pl.ds(2 * co, 2)], AF.at[j, pl.ds(2 * co, 2)], ad_s.at[j], ad_r.at[j], partner)
+        return rcopy(MP.at[lax.rem(u, NP), pl.ds(2 * co, 2)], MR1.at[j], m1_s.at[lax.rem(u, NP)], m1_r.at[lax.rem(u, NP)], partner)
+
+    def m2_copy(u, j):
+        return rcopy(MXS.at[j], MR2.at[j], m2_s.at[lax.rem(u, 4)], m2_r.at[j], xpeer)
+
+    def ax_copy(u, j):
+        return rcopy(AF.at[j, 2 * c + xx], AF.at[j, 2 * c + xx], ax_s.at[lax.rem(u, 4)], ax_r.at[j], xpeer)
+
+    def ax_recv(u, j):
+        return rcopy(AF.at[j, 2 * c + xo], AF.at[j, 2 * c + xo], ax_s.at[lax.rem(u, 4)], ax_r.at[j], xpeer)
+
+    def ad_copy(u, j):
+        return rcopy(AF.at[j, pl.ds(2 * c, 2)], AF.at[j, pl.ds(2 * c, 2)], ad_s.at[lax.rem(u, 3)], ad_r.at[j], partner)
+
+    def ad_recv(u, j):
+        return rcopy(AF.at[j, pl.ds(2 * co, 2)], AF.at[j, pl.ds(2 * co, 2)], ad_s.at[lax.rem(u, 3)], ad_r.at[j], partner)
 
     def dy_copy():
         return rcopy(DS, DR, dy_s.at[0], dy_r.at[0], ypeer)
@@ -332,10 +342,10 @@
     def stage0(u):
         half, j = lax.div(u, NJ), lax.rem(u, NJ)
 
-        @pl.when(u < NJ)
-        def _():
-            gu_load(j, 0).wait()
-            gu_load(j, 1).wait()
+        for first, last, sem in ((0, 2, 5), (2, 7, 6), (7, 9, 7)):
+            @pl.when(u == first)
+            def _(first=first, last=last, sem=sem):
+                await_all(WA.at[pl.ds(2 * first, 2 * (last - first))], sem)
 
         slot = lax.rem(u, NP)
         n = NB[1 - half]
@@ -349,32 +359,31 @@
         j, slot = lax.rem(u, NJ), lax.rem(u, NP)
         m1_copy(u, j).wait_recv()
         MXS[j] = (MP[slot, 2 * c + xo].astype(f32) + MR1[j, xo].astype(f32)).astype(bf16)
-        m2_copy(j).start()
+        m2_copy(u, j).start()
 
     def stage2(u):
         j, slot = lax.rem(u, NJ), lax.rem(u, NP)
         m1_copy(u, j).wait_send()
-        m2_copy(j).wait_recv()
+        m2_copy(u, j).wait()
         tot = (MP[slot, 2 * c + xx].astype(f32) + MR1[j, xx].astype(f32) + MR2[j].astype(f32)).astype(bf16).astype(f32)
         gate, up = tot[0], tot[1]
         AF[j, 2 * c + xx] = (gate * jax.nn.sigmoid(gate) * up).astype(bf16)
-        ax_copy(j).start()
+        ax_copy(u, j).start()
 
     def stage3(u):
         j = lax.rem(u, NJ)
-        m2_copy(j).wait_send()
-        ax_recv(j).wait_recv()
-        ad_copy(j).start()
+        ax_copy(u, j).wait_send()
+        ax_recv(u, j).wait_recv()
+        ad_copy(u, j).start()
 
     def stage4(u):
         j = lax.rem(u, NJ)
-        ax_copy(j).wait_send()
-
-        @pl.when(u < NJ)
-        def _():
-            wd_load(j).wait()
-
-        ad_recv(j).wait_recv()
+
+        @pl.when(u == 0)
+        def _():
+            wd_load().wait()
+
+        ad_recv(u, j).wait_recv()
         a = jnp.concatenate([AF[j, b] for b in range(4)], axis=0)
         prod = bdot(a, WB[pl.ds(pl.multiple_of(j * CH, CH), CH), :])
 
@@ -386,7 +395,7 @@
         def _():
             ACC[...] += prod
 
-        ad_copy(j).wait_send()
+        ad_copy(u, j).wait_send()
 
         @pl.when(u == NJ - 1)
         def _():
@@ -421,10 +430,7 @@
     AO[0] = (HB[0].astype(f32) + mlp.astype(f32)).astype(bf16)
     y_store = pltpu.make_async_copy(AO.at[0], y_hbm, lsem.at[0])
     y_store.start()
-    for k in range(1, 4):
-        st1_copy(0, k).wait_send()
-    for k in range(4):
-        st1_copy(1, k).wait_send()
+    st1_all(1, 7, 0).wait_send()
     x_send.wait_send()
     for r in range(2):
         for m in range(3):
@@ -438,8 +444,7 @@
             od_copy(r, p).wait_send()
         if r == 1:
             ay_copy(r).wait_send()
-        for k in range(1, 4):
-            st2_copy(r, k).wait_send()
+        st2_all(r).wait_send()
     dy_copy().wait_send()
     y_store.wait()
 
@@ -454,7 +459,7 @@
         vm((2, S, D1), bf16),
         vm((2, S, D1), bf16),
         vm((2, S, D1), bf16),
-        vm((2, 4, 8, 128), f32),
+        vm((8, 8, 128), f32),
         vm((2, 4, 8, 128), f32),
         vm((3, 2, S, GW), bf16),
         vm((2, 3, 2, S, GW), bf16),
@@ -475,12 +480,12 @@
         vm((S, HEAD_DIM), f32),
         vm((S, HEAD_DIM), f32),
         vm((GH, S, S), bf16),
-        dma((37,)), dma((3,)), dma((1,)), dma((1,)),
-        dma((2, 4)), dma((2, 4)), dma((2, 4)), dma((2, 4)),
-        dma((2, 3)), dma((2, 3)), dma((2, 4)), dma((2, 4)),
+        dma((9,)), dma((3,)), dma((1,)), dma((1,)),
+        dma((1,)), dma((2,)), dma((2,)), dma((2,)),
+        dma((3,)), dma((2, 3)), dma((4,)), dma((7,)),
         dma((3,)), dma((3,)), dma((3,)), dma((3,)), dma((2,)), dma((2,)),
-        dma((NJ,)), dma((NJ,)), dma((NJ,)), dma((NJ,)),
-        dma((NJ,)), dma((NJ,)), dma((NJ,)), dma((NJ,)), dma((1,)), dma((1,)),
+        dma((NP,)), dma((NP,)), dma((4,)), dma((NJ,)),
+        dma((4,)), dma((NJ,)), dma((3,)), dma((NJ,)), dma((1,)), dma((1,)),
     ]
     y = pl.pallas_call(
         kernel,

time: 73.1 us -> 70.2 us (0.960)
  Pallas kernels: 71.4 us -> 68.5 us
    pallas_call x1, Pallas kernels: 71.4 us -> 68.5 us  [layer_fn(): pl.pallas_call(kernel, out_shape=jax.ShapeDtypeStruct((S, D1), bf16), in_...]
where the time goes in v5:
time: 70.2 us; the launch traced here: 70.1 us
  Pallas kernels  68.5 us (98%)
  local copies, waits for them, and re-layouts  1.59 us (2%)
    pallas_call x1, Pallas kernels, layer_fn(): pl.pallas_call(kernel, out_shape=jax.ShapeDtypeStruct((S, D1), bf16), in_...  68.5 us
    unnamed x1, local copies, waits for them, and re-layouts  1.59 us

profile of v5, /device:TPU:0, one launch (start us, length us, event | category | flops | bytes accessed | tf_op | source)
XLA Modules:
  0.0 70.1 jit_solution(15712565134639615023)
XLA Ops:
  0.0 68.5 %shard_map.100 = bf16[64,1280]{1,0:T(8,128)(2,1)} custom-call(bf16[64,1280]{1,0:T(8,128)(2,1)} %bitcast.3, bf16[1280,2560]{1,0:T(8,128)(2,1)} %wq.1, bf16[1280,2560]{1,0:T(8,128)(2,1)} %wk.1, bf16[1280,2560]{1,0:T(8,128)(2,1)} %wv.1, bf16[2560,1280]{1,0:T(8,128)(2,1)} %wo.1, bf16[1280,6912]{1,0:T(8,128)(2,1)} %wg.1, bf16[1280,6912]{1,0:T(8,128)(2,1)} %wu.1, ...), custom_call_target="tpu_custom_call" | custom-call | tf_op jit(solution)/shard_map/pallas_call | solution.py:490
  68.5 1.6 %copy.12 = bf16[1,64,1280]{2,1,0:T(8,128)(2,1)} copy(bf16[1,64,1280]{2,1,0:T(8,128)(2,1)} %bitcast.2) | data formatting | bytes 327680

commit v6 on v5

--- a/solution.py
+++ b/solution.py
@@ -40,11 +40,11 @@
 
 
 def kernel(
-    x_hbm, wq, wk, wv, wo, wg, wu, wd, cos_hbm, sin_hbm, y_hbm,
+    x_hbm, wq, wk, wv, wo, wg, wu, wd, cos_hbm, sin_hbm, h_hbm, m_hbm,
     WA, WB, XB, NB, HB, ST1, ST2, PS, PO, R1, XS, R2, OF, AO, AR,
     MP, MR1, MXS, MR2, AF, ACC, DS, DR, COS, SIN, PR,
     wsem, lsem, xg_s, xg_r, st1_s, st1_r, st2_s, st2_r,
-    q1_s, q1_r, q2_s, q2_r, ox_s, ox_r, od_s, od_r, ay_s, ay_r,
+    q1_s, q1_r, q2_s, q2_r, ox_s, ox_r, od_s, od_r, ob_s, ob_r, ay_s, ay_r,
     m1_s, m1_r, m2_s, m2_r, ax_s, ax_r, ad_s, ad_r, dy_s, dy_r,
 ):
     f32, bf16 = jnp.float32, jnp.bfloat16
@@ -69,8 +69,7 @@
     barrier = pltpu.get_barrier_semaphore()
     for k in range(1, 4):
         pl.semaphore_signal(barrier, inc=1, device_id={"tx": lax.rem(tx + k, 4)}, device_id_type=MESH)
-    for k in range(4):
-        pl.semaphore_signal(barrier, inc=1, device_id={"ty": tyo, "tx": lax.rem(tx + k, 4)}, device_id_type=MESH)
+    pl.semaphore_signal(barrier, inc=1, device_id=ypeer, device_id_type=MESH)
 
     def qkv_load(m, half):
         src = (wq, wk, wv)[m].at[:, pl.ds(half * D1, D1)]
@@ -119,22 +118,22 @@
     x_load.wait()
     x_own = XB[0].astype(f32)
     ST1[0] = stats_tile(x_own)
-    pl.semaphore_wait(barrier, 7)
-
-    def st1_copy(r, k):
-        dev = {"tx": lax.rem(tx + k, 4)} if r == 0 else {"ty": tyo, "tx": lax.rem(tx + k, 4)}
-        return rcopy(ST1.at[0], ST1.at[4 * r + k], st1_s.at[0], st1_r.at[r], dev)
-
-    def st1_all(first, count, r):
-        ref = ST1.at[pl.ds(first, count)]
-        return rcopy(ref, ref, st1_s.at[0], st1_r.at[r], partner)
+    pl.semaphore_wait(barrier, 4)
+
+    def st1_copy(k):
+        return rcopy(ST1.at[0], ST1.at[k], st1_s.at[0], st1_r.at[0], {"tx": lax.rem(tx + k, 4)})
+
+    def st1_all():
+        ref = ST1.at[pl.ds(1, 3)]
+        return rcopy(ref, ref, st1_s.at[0], st1_r.at[0], partner)
+
+    def st1_total():
+        return rcopy(ST1.at[4], ST1.at[5], st1_s.at[1], st1_r.at[1], ypeer)
 
     for k in range(1, 4):
-        st1_copy(0, k).start()
+        st1_copy(k).start()
     x_send = rcopy(XB.at[0], XB.at[1], xg_s.at[0], xg_r.at[0], ypeer)
     x_send.start()
-    for k in range(4):
-        st1_copy(1, k).start()
 
     def q1_copy(r, m):
         return rcopy(PS.at[m], R1.at[r, m], q1_s.at[m], q1_r.at[r, m], partner)
@@ -182,21 +181,30 @@
     def o_lanes(r, p):
         return pl.ds(*(PARTS[p] if r == 1 else (0, GW)))
 
-    def ox_copy(r, p=0):
-        ref = OF.at[r, c, xx, :, o_lanes(r, p)]
-        return rcopy(ref, ref, ox_s.at[r + p], ox_r.at[r + p], xpeer)
-
-    def ox_recv(r, p=0):
-        ref = OF.at[r, c, xo, :, o_lanes(r, p)]
-        return rcopy(ref, ref, ox_s.at[r + p], ox_r.at[r + p], xpeer)
-
-    def od_copy(r, p=0):
-        ref = OF.at[r, c, :, :, o_lanes(r, p)]
-        return rcopy(ref, ref, od_s.at[r + p], od_r.at[r + p], partner)
-
-    def od_recv(r, p=0):
-        ref = OF.at[r, co, :, :, o_lanes(r, p)]
-        return rcopy(ref, ref, od_s.at[r + p], od_r.at[r + p], partner)
+    def ox_copy(r):
+        ref = OF.at[r, c, xx, :, o_lanes(r, 0)]
+        return rcopy(ref, ref, ox_s.at[r], ox_r.at[r], xpeer)
+
+    def ox_recv(r):
+        ref = OF.at[r, c, xo, :, o_lanes(r, 0)]
+        return rcopy(ref, ref, ox_s.at[r], ox_r.at[r], xpeer)
+
+    def od_copy(r):
+        ref = OF.at[r, c, :, :, o_lanes(r, 0)]
+        return rcopy(ref, ref, od_s.at[r], od_r.at[r], partner)
+
+    def od_recv(r):
+        ref = OF.at[r, co, :, :, o_lanes(r, 0)]
+        return rcopy(ref, ref, od_s.at[r], od_r.at[r], partner)
+
+    def ob_copy(k):
+        ref = OF.at[1, c, xx, :, o_lanes(1, 1)]
+        return rcopy(ref, ref, ob_s.at[k - 1], ob_r.at[k - 1], {"tx": lax.rem(tx + k, 4)})
+
+    def ob_recv(k):
+        src = lax.rem(tx + 4 - k, 4)
+        ref = OF.at[1, lax.rem(src, 2), lax.div(src, 2), :, o_lanes(1, 1)]
+        return rcopy(ref, ref, ob_s.at[k - 1], ob_r.at[k - 1], partner)
 
     def total(r, m, lanes):
         return (PO[r, m, xx, :, lanes].astype(f32) + R1[r, m, xx, :, lanes].astype(f32) + R2[r, m, :, lanes].astype(f32)).astype(bf16)
@@ -226,11 +234,15 @@
         heads = range(off // HEAD_DIM, (off + size) // HEAD_DIM)
         outs = [bdot(PR[h], total(r, 2, pl.ds(h * HEAD_DIM, HEAD_DIM))).astype(bf16) for h in heads]
         OF[r, c, xx, :, off:off + size] = jnp.concatenate(outs, axis=1)
-        ox_copy(r, p).start()
-
-    def o_forward(r, p=0):
-        ox_recv(r, p).wait_recv()
-        od_copy(r, p).start()
+        if p == 0:
+            ox_copy(r).start()
+        else:
+            for k in (2, 1, 3):
+                ob_copy(k).start()
+
+    def o_forward(r):
+        ox_recv(r).wait_recv()
+        od_copy(r).start()
 
     def ay_copy(r):
         return rcopy(AO.at[r], AR.at[1 - r], ay_s.at[r], ay_r.at[1 - r], ypeer)
@@ -243,6 +255,8 @@
         if r == 0:
             await_all(WA.at[pl.ds(14, 2)], 3)
             await_all(WA.at[pl.ds(16, 2), :, pl.ds(0, D1 - CH)], 4)
+        if r == 1:
+            ob_recv(2).wait_recv()
         lo, hi = out_half(r, c)
         ACC[:, :CH] = lo
         ACC[:, CH:] = hi
@@ -250,14 +264,18 @@
     def out_rest(r):
         od_recv(r).wait_recv()
         if r == 1:
-            od_recv(r, 1).wait_recv()
+            ob_recv(1).wait_recv()
+            ob_recv(3).wait_recv()
         lo, hi = out_half(r, co)
         AO[r, :, :CH] = (ACC[:, :CH] + lo).astype(bf16)
         AO[r, :, CH:] = (ACC[:, CH:] + hi).astype(bf16)
         ay_copy(r).start()
 
-    st1_all(1, 3, 0).wait_recv()
-    NB[0] = normalize(x_own, ST1[0] + ST1[1] + ST1[2] + ST1[3])
+    st1_all().wait_recv()
+    sums = ST1[0] + ST1[1] + ST1[2] + ST1[3]
+    ST1[4] = sums
+    st1_total().start()
+    NB[0] = normalize(x_own, sums)
     qkv_mm(0, 0)
     qkv_s1(0, 0)
     qkv_mm(0, 1)
@@ -269,8 +287,8 @@
         gu_load(j, 0).start()
         gu_load(j, 1).start()
     x_send.wait_recv()
-    st1_all(4, 4, 1).wait_recv()
-    NB[1] = normalize(XB[1].astype(f32), ST1[4] + ST1[5] + ST1[6] + ST1[7])
+    st1_total().wait_recv()
+    NB[1] = normalize(XB[1].astype(f32), ST1[5])
     qkv_s1(0, 2)
     qkv_mm(1, 0)
     qkv_s1(1, 0)
@@ -287,8 +305,7 @@
     out_rest(0)
     values(1, 0)
     values(1, 1)
-    o_forward(1, 0)
-    o_forward(1, 1)
+    o_forward(1)
     out_own(1)
     out_rest(1)
     for j in range(7, NJ):
@@ -424,13 +441,16 @@
 
     lax.fori_loop(0, NU + L4, step, 0)
 
+    h_store = pltpu.make_async_copy(HB.at[0], h_hbm, lsem.at[1])
+    h_store.start()
     dy_copy().wait_recv()
     mlp = (ACC[...] + DR[...].astype(f32)).astype(bf16)
     ay_copy(0).wait_send()
-    AO[0] = (HB[0].astype(f32) + mlp.astype(f32)).astype(bf16)
-    y_store = pltpu.make_async_copy(AO.at[0], y_hbm, lsem.at[0])
-    y_store.start()
-    st1_all(1, 7, 0).wait_send()
+    AO[0] = mlp
+    m_store = pltpu.make_async_copy(AO.at[0], m_hbm, lsem.at[0])
+    m_store.start()
+    st1_all().wait_send()
+    st1_total().wait_send()
     x_send.wait_send()
     for r in range(2):
         for m in range(3):
@@ -439,14 +459,16 @@
                 q2_copy(r, m).wait_send()
         if r == 1:
             q2_copy(1, 2, 1).wait_send()
-        for p in range(r + 1):
-            ox_copy(r, p).wait_send()
-            od_copy(r, p).wait_send()
+            for k in range(1, 4):
+                ob_copy(k).wait_send()
+        ox_copy(r).wait_send()
+        od_copy(r).wait_send()
         if r == 1:
             ay_copy(r).wait_send()
         st2_all(r).wait_send()
     dy_copy().wait_send()
-    y_store.wait()
+    h_store.wait()
+    m_store.wait()
 
 
 def layer_fn(x_blk, w_q, w_k, w_v, w_o, w_gate, w_up, w_down):
@@ -459,7 +481,7 @@
         vm((2, S, D1), bf16),
         vm((2, S, D1), bf16),
         vm((2, S, D1), bf16),
-        vm((8, 8, 128), f32),
+        vm((6, 8, 128), f32),
         vm((2, 4, 8, 128), f32),
         vm((3, 2, S, GW), bf16),
         vm((2, 3, 2, S, GW), bf16),
@@ -481,21 +503,21 @@
         vm((S, HEAD_DIM), f32),
         vm((GH, S, S), bf16),
         dma((9,)), dma((3,)), dma((1,)), dma((1,)),
-        dma((1,)), dma((2,)), dma((2,)), dma((2,)),
+        dma((2,)), dma((2,)), dma((2,)), dma((2,)),
         dma((3,)), dma((2, 3)), dma((4,)), dma((7,)),
-        dma((3,)), dma((3,)), dma((3,)), dma((3,)), dma((2,)), dma((2,)),
+        dma((2,)), dma((2,)), dma((2,)), dma((2,)), dma((3,)), dma((3,)), dma((2,)), dma((2,)),
         dma((NP,)), dma((NP,)), dma((4,)), dma((NJ,)),
         dma((4,)), dma((NJ,)), dma((3,)), dma((NJ,)), dma((1,)), dma((1,)),
     ]
-    y = pl.pallas_call(
+    h, mlp = pl.pallas_call(
         kernel,
-        out_shape=jax.ShapeDtypeStruct((S, D1), bf16),
+        out_shape=[jax.ShapeDtypeStruct((S, D1), bf16)] * 2,
         in_specs=[pl.BlockSpec(memory_space=pl.ANY)] * 10,
-        out_specs=pl.BlockSpec(memory_space=pl.ANY),
+        out_specs=[pl.BlockSpec(memory_space=pl.ANY)] * 2,
         scratch_shapes=scratch,
         compiler_params=pltpu.CompilerParams(collective_id=0, has_side_effects=True, vmem_limit_bytes=67_043_328),
     )(x_blk.reshape(S, D1), w_q, w_k, w_v, w_o, w_gate, w_up, w_down, jnp.asarray(cos_t), jnp.asarray(sin_t))
-    return y.reshape(x_blk.shape)
+    return (h.astype(f32) + mlp.astype(f32)).astype(bf16).reshape(x_blk.shape)
 
 
 def solution(mesh):

time: 70.2 us -> 70.1 us (level)
  other arithmetic: 0 us -> 1.7 us
  local copies, waits for them, and re-layouts: 1.59 us -> 0 us
    reshape x0 -> x1, other arithmetic: none -> 1.7 us  [layer_fn(): return (h.astype(f32) + mlp.astype(f32)).astype(bf16).reshape(x_blk.shape)]
    unnamed x1 -> x0, local copies, waits for them, and re-layouts: 1.59 us -> none
where the time goes in v6:
time: 70.1 us; the launch traced here: 70 us
  Pallas kernels  68.3 us (97%)
  other arithmetic  1.7 us (2%)
    pallas_call x1, Pallas kernels, layer_fn(): pl.pallas_call(kernel, out_shape=[jax.ShapeDtypeStruct((S, D1), bf16)] *...  68.3 us
    reshape x1, other arithmetic, layer_fn(): return (h.astype(f32) + mlp.astype(f32)).astype(bf16).reshape(x_blk.shape)  1.7 us

profile of v6, /device:TPU:0, one launch (start us, length us, event | category | flops | bytes accessed | tf_op | source)
XLA Modules:
  0.0 70.0 jit_solution(9234753902868272856)
XLA Ops:
  0.0 68.3 %shard_map.100 = (bf16[64,1280]{1,0:T(8,128)(2,1)}, bf16[64,1280]{1,0:T(8,128)(2,1)}) custom-call(bf16[64,1280]{1,0:T(8,128)(2,1)} %bitcast.3, bf16[1280,2560]{1,0:T(8,128)(2,1)} %wq.1, bf16[1280,2560]{1,0:T(8,128)(2,1)} %wk.1, bf16[1280,2560]{1,0:T(8,128)(2,1)} %wv.1, bf16[2560,1280]{1,0:T(8,128)(2,1)} %wo.1, bf16[1280,6912]{1,0:T(8,128)(2,1)} %wg.1, ...), custom_call_target="tpu_custom_call" | custom-call | tf_op jit(solution)/shard_map/pallas_call | solution.py:512
  68.3 1.7 %fusion = bf16[1,64,1280]{2,1,0:T(8,128)(2,1)} fusion(bf16[64,1280]{1,0:T(8,128)(2,1)} %get-tuple-element.8, bf16[64,1280]{1,0:T(8,128)(2,1)} %get-tuple-element.7), kind=kLoop, calls=%fused_computation.1 | loop fusion | flops 327680 | bytes 491520 | tf_op jit(solution)/shard_map/reshape | solution.py:520

commit v7 on v6

--- a/solution.py
+++ b/solution.py
@@ -21,9 +21,10 @@
 CH = 768
 NJ = 9
 NU = 2 * NJ
-NP = 5
+NP = 3
 PARTS = ((0, 384), (384, 256))
 L1, L2, L3, L4 = 1, 4, 7, 9
+LATE = 13
 
 
 def rotary_tables():
@@ -244,12 +245,12 @@
         ox_recv(r).wait_recv()
         od_copy(r).start()
 
-    def ay_copy(r):
-        return rcopy(AO.at[r], AR.at[1 - r], ay_s.at[r], ay_r.at[1 - r], ypeer)
-
-    def out_half(r, half):
-        o = jnp.concatenate([OF[r, half, 0], OF[r, half, 1]], axis=1)
-        return bdot(o, WA[14 + half]), bdot(o, WA[16 + half, :, : D1 - CH])
+    def ay_copy(r, p):
+        cols = pl.ds(*((0, CH), (CH, D1 - CH))[p])
+        return rcopy(AO.at[r, :, cols], AR.at[1 - r, :, cols], ay_s.at[r, p], ay_r.at[1 - r, p], ypeer)
+
+    def heads_of(r, half):
+        return jnp.concatenate([OF[r, half, 0], OF[r, half, 1]], axis=1)
 
     def out_own(r):
         if r == 0:
@@ -257,19 +258,20 @@
             await_all(WA.at[pl.ds(16, 2), :, pl.ds(0, D1 - CH)], 4)
         if r == 1:
             ob_recv(2).wait_recv()
-        lo, hi = out_half(r, c)
-        ACC[:, :CH] = lo
-        ACC[:, CH:] = hi
+        o = heads_of(r, c)
+        ACC[:, :CH] = bdot(o, WA[14 + c])
+        ACC[:, CH:] = bdot(o, WA[16 + c, :, : D1 - CH])
 
     def out_rest(r):
         od_recv(r).wait_recv()
         if r == 1:
             ob_recv(1).wait_recv()
             ob_recv(3).wait_recv()
-        lo, hi = out_half(r, co)
-        AO[r, :, :CH] = (ACC[:, :CH] + lo).astype(bf16)
-        AO[r, :, CH:] = (ACC[:, CH:] + hi).astype(bf16)
-        ay_copy(r).start()
+        o = heads_of(r, co)
+        AO[r, :, :CH] = (ACC[:, :CH] + bdot(o, WA[14 + co])).astype(bf16)
+        ay_copy(r, 0).start()
+        AO[r, :, CH:] = (ACC[:, CH:] + bdot(o, WA[16 + co, :, : D1 - CH])).astype(bf16)
+        ay_copy(r, 1).start()
 
     st1_all().wait_recv()
     sums = ST1[0] + ST1[1] + ST1[2] + ST1[3]
@@ -301,8 +303,8 @@
     qkv_s1(1, 2)
     o_forward(0)
     out_own(0)
+    out_rest(0)
     scores(1)
-    out_rest(0)
     values(1, 0)
     values(1, 1)
     o_forward(1)
@@ -320,7 +322,8 @@
         return rcopy(ref, ref, st2_s.at[r], st2_r.at[r], partner)
 
     def residual(r):
-        ay_copy(1 - r).wait_recv()
+        ay_copy(1 - r, 0).wait_recv()
+        ay_copy(1 - r, 1).wait_recv()
         attn = (AO[r].astype(f32) + AR[r].astype(f32)).astype(bf16)
         h = (XB[r].astype(f32) + attn.astype(f32)).astype(bf16)
         HB[r] = h
@@ -336,16 +339,16 @@
     norm2(1)
 
     def m1_copy(u, j):
-        return rcopy(MP.at[lax.rem(u, NP), pl.ds(2 * co, 2)], MR1.at[j], m1_s.at[lax.rem(u, NP)], m1_r.at[lax.rem(u, NP)], partner)
+        return rcopy(MP.at[lax.rem(u, NP), pl.ds(2 * co, 2)], MR1.at[j], m1_s.at[lax.rem(u, NP)], m1_r.at[lax.rem(u, 5)], partner)
 
     def m2_copy(u, j):
-        return rcopy(MXS.at[j], MR2.at[j], m2_s.at[lax.rem(u, 4)], m2_r.at[j], xpeer)
+        return rcopy(MXS.at[j], MR2.at[u], m2_s.at[j], m2_r.at[u], xpeer)
 
     def ax_copy(u, j):
-        return rcopy(AF.at[j, 2 * c + xx], AF.at[j, 2 * c + xx], ax_s.at[lax.rem(u, 4)], ax_r.at[j], xpeer)
+        return rcopy(AF.at[j, 2 * c + xx], AF.at[j, 2 * c + xx], ax_s.at[j], ax_r.at[j], xpeer)
 
     def ax_recv(u, j):
-        return rcopy(AF.at[j, 2 * c + xo], AF.at[j, 2 * c + xo], ax_s.at[lax.rem(u, 4)], ax_r.at[j], xpeer)
+        return rcopy(AF.at[j, 2 * c + xo], AF.at[j, 2 * c + xo], ax_s.at[j], ax_r.at[j], xpeer)
 
     def ad_copy(u, j):
         return rcopy(AF.at[j, pl.ds(2 * c, 2)], AF.at[j, pl.ds(2 * c, 2)], ad_s.at[lax.rem(u, 3)], ad_r.at[j], partner)
@@ -377,12 +380,13 @@
         m1_copy(u, j).wait_recv()
         MXS[j] = (MP[slot, 2 * c + xo].astype(f32) + MR1[j, xo].astype(f32)).astype(bf16)
         m2_copy(u, j).start()
+        MR1[j, xx] = (MP[slot, 2 * c + xx].astype(f32) + MR1[j, xx].astype(f32)).astype(bf16)
+        m1_copy(u, j).wait_send()
 
     def stage2(u):
-        j, slot = lax.rem(u, NJ), lax.rem(u, NP)
-        m1_copy(u, j).wait_send()
+        j = lax.rem(u, NJ)
         m2_copy(u, j).wait()
-        tot = (MP[slot, 2 * c + xx].astype(f32) + MR1[j, xx].astype(f32) + MR2[j].astype(f32)).astype(bf16).astype(f32)
+        tot = (MR1[j, xx].astype(f32) + MR2[u].astype(f32)).astype(bf16).astype(f32)
         gate, up = tot[0], tot[1]
         AF[j, 2 * c + xx] = (gate * jax.nn.sigmoid(gate) * up).astype(bf16)
         ax_copy(u, j).start()
@@ -432,20 +436,50 @@
         def _():
             stage0(t)
 
-        for lag, stage in ((L1, stage1), (L2, stage2), (L3, stage3), (L4, stage4)):
-            @pl.when((t >= lag) & (t < NU + lag))
-            def _(lag=lag, stage=stage):
-                stage(t - lag)
+        @pl.when((t >= L1) & (t < NU + L1))
+        def _():
+            stage1(t - L1)
+
+        @pl.when((t >= L2) & (t < LATE))
+        def _():
+            stage2(t - L2)
+
+        @pl.when(t == NU)
+        def _():
+            lax.fori_loop(LATE - L2, NU - L2, lambda u, x: (stage2(u), x)[1], 0)
+
+        @pl.when((t >= NU) & (t < NU + L2))
+        def _():
+            stage2(t - L2)
+
+        @pl.when((t >= L3) & (t < LATE - L2 + L3))
+        def _():
+            stage3(t - L3)
+
+        @pl.when(t >= NU)
+        def _():
+            @pl.when(t < NU + LATE - L2)
+            def _():
+                stage3(t - (LATE - L2))
+
+        @pl.when((t >= L4) & (t < NU))
+        def _():
+            stage4(t - L4)
+
+        @pl.when(t > NU)
+        def _():
+            stage4(t - L4 - 1)
 
         return carry
 
-    lax.fori_loop(0, NU + L4, step, 0)
+    lax.fori_loop(0, NU + L4 + 1, step, 0)
 
     h_store = pltpu.make_async_copy(HB.at[0], h_hbm, lsem.at[1])
     h_store.start()
     dy_copy().wait_recv()
     mlp = (ACC[...] + DR[...].astype(f32)).astype(bf16)
-    ay_copy(0).wait_send()
+    ay_copy(0, 0).wait_send()
+    ay_copy(0, 1).wait_send()
     AO[0] = mlp
     m_store = pltpu.make_async_copy(AO.at[0], m_hbm, lsem.at[0])
     m_store.start()
@@ -464,7 +498,8 @@
         ox_copy(r).wait_send()
         od_copy(r).wait_send()
         if r == 1:
-            ay_copy(r).wait_send()
+            ay_copy(r, 0).wait_send()
+            ay_copy(r, 1).wait_send()
         st2_all(r).wait_send()
     dy_copy().wait_send()
     h_store.wait()
@@ -494,7 +529,7 @@
         vm((NP, 4, 2, 16, CH), bf16),
         vm((NJ, 2, 2, 16, CH), bf16),
         vm((NJ, 2, 16, CH), bf16),
-        vm((NJ, 2, 16, CH), bf16),
+        vm((NU, 2, 16, CH), bf16),
         vm((NJ, 4, 16, CH), bf16),
         vm((S, D1), f32),
         vm((S, D1), bf16),
@@ -505,9 +540,9 @@
         dma((9,)), dma((3,)), dma((1,)), dma((1,)),
         dma((2,)), dma((2,)), dma((2,)), dma((2,)),
         dma((3,)), dma((2, 3)), dma((4,)), dma((7,)),
-        dma((2,)), dma((2,)), dma((2,)), dma((2,)), dma((3,)), dma((3,)), dma((2,)), dma((2,)),
-        dma((NP,)), dma((NP,)), dma((4,)), dma((NJ,)),
-        dma((4,)), dma((NJ,)), dma((3,)), dma((NJ,)), dma((1,)), dma((1,)),
+        dma((2,)), dma((2,)), dma((2,)), dma((2,)), dma((3,)), dma((3,)), dma((2, 2)), dma((2, 2)),
+        dma((NP,)), dma((5,)), dma((NJ,)), dma((NU,)),
+        dma((NJ,)), dma((NJ,)), dma((3,)), dma((NJ,)), dma((1,)), dma((1,)),
     ]
     h, mlp = pl.pallas_call(
         kernel,

time: 70.1 us -> 72.5 us (1.034)
  Pallas kernels: 68.3 us -> 70.7 us
    pallas_call x1, Pallas kernels: 68.3 us -> 70.7 us  [layer_fn(): pl.pallas_call(kernel, out_shape=[jax.ShapeDtypeStruct((S, D1), bf16)] *...]
where the time goes in v7:
time: 72.5 us; the launch traced here: 72.4 us
  Pallas kernels  70.7 us (98%)
  other arithmetic  1.7 us (2%)
    pallas_call x1, Pallas kernels, layer_fn(): pl.pallas_call(kernel, out_shape=[jax.ShapeDtypeStruct((S, D1), bf16)] *...  70.7 us
    reshape x1, other arithmetic, layer_fn(): return (h.astype(f32) + mlp.astype(f32)).astype(bf16).reshape(x_blk.shape)  1.7 us

profile of v7, /device:TPU:0, one launch (start us, length us, event | category | flops | bytes accessed | tf_op | source)
XLA Modules:
  0.0 72.4 jit_solution(4146104445755684280)
XLA Ops:
  0.0 70.7 %shard_map.100 = (bf16[64,1280]{1,0:T(8,128)(2,1)}, bf16[64,1280]{1,0:T(8,128)(2,1)}) custom-call(bf16[64,1280]{1,0:T(8,128)(2,1)} %bitcast.3, bf16[1280,2560]{1,0:T(8,128)(2,1)} %wq.1, bf16[1280,2560]{1,0:T(8,128)(2,1)} %wk.1, bf16[1280,2560]{1,0:T(8,128)(2,1)} %wv.1, bf16[2560,1280]{1,0:T(8,128)(2,1)} %wo.1, bf16[1280,6912]{1,0:T(8,128)(2,1)} %wg.1, ...), custom_call_target="tpu_custom_call" | custom-call | tf_op jit(solution)/shard_map/pallas_call | solution.py:547
  70.7 1.7 %fusion = bf16[1,64,1280]{2,1,0:T(8,128)(2,1)} fusion(bf16[64,1280]{1,0:T(8,128)(2,1)} %get-tuple-element.8, bf16[64,1280]{1,0:T(8,128)(2,1)} %get-tuple-element.7), kind=kLoop, calls=%fused_computation.1 | loop fusion | flops 327680 | bytes 491520 | tf_op jit(solution)/shard_map/reshape | solution.py:555

commit v8 on v7

--- a/solution.py
+++ b/solution.py
@@ -24,7 +24,6 @@
 NP = 3
 PARTS = ((0, 384), (384, 256))
 L1, L2, L3, L4 = 1, 4, 7, 9
-LATE = 13
 
 
 def rotary_tables():
@@ -43,10 +42,10 @@
 def kernel(
     x_hbm, wq, wk, wv, wo, wg, wu, wd, cos_hbm, sin_hbm, h_hbm, m_hbm,
     WA, WB, XB, NB, HB, ST1, ST2, PS, PO, R1, XS, R2, OF, AO, AR,
-    MP, MR1, MXS, MR2, AF, ACC, DS, DR, COS, SIN, PR,
+    MP, MR1, MXS, MR2, AF, AZ, ACC, DS, DR, COS, SIN, PR,
     wsem, lsem, xg_s, xg_r, st1_s, st1_r, st2_s, st2_r,
-    q1_s, q1_r, q2_s, q2_r, ox_s, ox_r, od_s, od_r, ob_s, ob_r, ay_s, ay_r,
-    m1_s, m1_r, m2_s, m2_r, ax_s, ax_r, ad_s, ad_r, dy_s, dy_r,
+    q1_s, q1_r, q2_s, q2_r, ox_s, ox_r, od_s, od_r, ay_s, ay_r,
+    m1_s, m1_r, m2_s, m2_r, ax_s, ax_r, ad_s, ad_r, az_s, az_r, dy_s, dy_r,
 ):
     f32, bf16 = jnp.float32, jnp.bfloat16
     ty = lax.axis_index("ty")
@@ -182,30 +181,21 @@
     def o_lanes(r, p):
         return pl.ds(*(PARTS[p] if r == 1 else (0, GW)))
 
-    def ox_copy(r):
-        ref = OF.at[r, c, xx, :, o_lanes(r, 0)]
-        return rcopy(ref, ref, ox_s.at[r], ox_r.at[r], xpeer)
-
-    def ox_recv(r):
-        ref = OF.at[r, c, xo, :, o_lanes(r, 0)]
-        return rcopy(ref, ref, ox_s.at[r], ox_r.at[r], xpeer)
-
-    def od_copy(r):
-        ref = OF.at[r, c, :, :, o_lanes(r, 0)]
-        return rcopy(ref, ref, od_s.at[r], od_r.at[r], partner)
-
-    def od_recv(r):
-        ref = OF.at[r, co, :, :, o_lanes(r, 0)]
-        return rcopy(ref, ref, od_s.at[r], od_r.at[r], partner)
-
-    def ob_copy(k):
-        ref = OF.at[1, c, xx, :, o_lanes(1, 1)]
-        return rcopy(ref, ref, ob_s.at[k - 1], ob_r.at[k - 1], {"tx": lax.rem(tx + k, 4)})
-
-    def ob_recv(k):
-        src = lax.rem(tx + 4 - k, 4)
-        ref = OF.at[1, lax.rem(src, 2), lax.div(src, 2), :, o_lanes(1, 1)]
-        return rcopy(ref, ref, ob_s.at[k - 1], ob_r.at[k - 1], partner)
+    def ox_copy(r, p=0):
+        ref = OF.at[r, c, xx, :, o_lanes(r, p)]
+        return rcopy(ref, ref, ox_s.at[r + p], ox_r.at[r + p], xpeer)
+
+    def ox_recv(r, p=0):
+        ref = OF.at[r, c, xo, :, o_lanes(r, p)]
+        return rcopy(ref, ref, ox_s.at[r + p], ox_r.at[r + p], xpeer)
+
+    def od_copy(r, p=0):
+        ref = OF.at[r, c, :, :, o_lanes(r, p)]
+        return rcopy(ref, ref, od_s.at[r + p], od_r.at[r + p], partner)
+
+    def od_recv(r, p=0):
+        ref = OF.at[r, co, :, :, o_lanes(r, p)]
+        return rcopy(ref, ref, od_s.at[r + p], od_r.at[r + p], partner)
 
     def total(r, m, lanes):
         return (PO[r, m, xx, :, lanes].astype(f32) + R1[r, m, xx, :, lanes].astype(f32) + R2[r, m, :, lanes].astype(f32)).astype(bf16)
@@ -235,15 +225,11 @@
         heads = range(off // HEAD_DIM, (off + size) // HEAD_DIM)
         outs = [bdot(PR[h], total(r, 2, pl.ds(h * HEAD_DIM, HEAD_DIM))).astype(bf16) for h in heads]
         OF[r, c, xx, :, off:off + size] = jnp.concatenate(outs, axis=1)
-        if p == 0:
-            ox_copy(r).start()
-        else:
-            for k in (2, 1, 3):
-                ob_copy(k).start()
-
-    def o_forward(r):
-        ox_recv(r).wait_recv()
-        od_copy(r).start()
+        ox_copy(r, p).start()
+
+    def o_forward(r, p=0):
+        ox_recv(r, p).wait_recv()
+        od_copy(r, p).start()
 
     def ay_copy(r, p):
         cols = pl.ds(*((0, CH), (CH, D1 - CH))[p])
@@ -256,8 +242,6 @@
         if r == 0:
             await_all(WA.at[pl.ds(14, 2)], 3)
             await_all(WA.at[pl.ds(16, 2), :, pl.ds(0, D1 - CH)], 4)
-        if r == 1:
-            ob_recv(2).wait_recv()
         o = heads_of(r, c)
         ACC[:, :CH] = bdot(o, WA[14 + c])
         ACC[:, CH:] = bdot(o, WA[16 + c, :, : D1 - CH])
@@ -265,8 +249,7 @@
     def out_rest(r):
         od_recv(r).wait_recv()
         if r == 1:
-            ob_recv(1).wait_recv()
-            ob_recv(3).wait_recv()
+            od_recv(r, 1).wait_recv()
         o = heads_of(r, co)
         AO[r, :, :CH] = (ACC[:, :CH] + bdot(o, WA[14 + co])).astype(bf16)
         ay_copy(r, 0).start()
@@ -307,7 +290,8 @@
     scores(1)
     values(1, 0)
     values(1, 1)
-    o_forward(1)
+    o_forward(1, 0)
+    o_forward(1, 1)
     out_own(1)
     out_rest(1)
     for j in range(7, NJ):
@@ -342,19 +326,27 @@
         return rcopy(MP.at[lax.rem(u, NP), pl.ds(2 * co, 2)], MR1.at[j], m1_s.at[lax.rem(u, NP)], m1_r.at[lax.rem(u, 5)], partner)
 
     def m2_copy(u, j):
-        return rcopy(MXS.at[j], MR2.at[u], m2_s.at[j], m2_r.at[u], xpeer)
+        return rcopy(MXS.at[lax.rem(u, 5)], MR2.at[j], m2_s.at[lax.rem(u, 5)], m2_r.at[j], xpeer)
 
     def ax_copy(u, j):
-        return rcopy(AF.at[j, 2 * c + xx], AF.at[j, 2 * c + xx], ax_s.at[j], ax_r.at[j], xpeer)
+        return rcopy(AF.at[j, 2 * c + xx], AF.at[j, 2 * c + xx], ax_s.at[lax.rem(u, 4)], ax_r.at[j], xpeer)
 
     def ax_recv(u, j):
-        return rcopy(AF.at[j, 2 * c + xo], AF.at[j, 2 * c + xo], ax_s.at[j], ax_r.at[j], xpeer)
+        return rcopy(AF.at[j, 2 * c + xo], AF.at[j, 2 * c + xo], ax_s.at[lax.rem(u, 4)], ax_r.at[j], xpeer)
 
     def ad_copy(u, j):
         return rcopy(AF.at[j, pl.ds(2 * c, 2)], AF.at[j, pl.ds(2 * c, 2)], ad_s.at[lax.rem(u, 3)], ad_r.at[j], partner)
 
     def ad_recv(u, j):
         return rcopy(AF.at[j, pl.ds(2 * co, 2)], AF.at[j, pl.ds(2 * co, 2)], ad_s.at[lax.rem(u, 3)], ad_r.at[j], partner)
+
+    def az_copy(k):
+        return rcopy(AZ.at[2 * c + xx], AZ.at[2 * c + xx], az_s.at[k - 1], az_r.at[k - 1], {"tx": lax.rem(tx + k, 4)})
+
+    def az_recv(k):
+        src = lax.rem(tx + 4 - k, 4)
+        block = AZ.at[2 * lax.rem(src, 2) + lax.div(src, 2)]
+        return rcopy(block, block, az_s.at[k - 1], az_r.at[k - 1], partner)
 
     def dy_copy():
         return rcopy(DS, DR, dy_s.at[0], dy_r.at[0], ypeer)
@@ -378,7 +370,7 @@
     def stage1(u):
         j, slot = lax.rem(u, NJ), lax.rem(u, NP)
         m1_copy(u, j).wait_recv()
-        MXS[j] = (MP[slot, 2 * c + xo].astype(f32) + MR1[j, xo].astype(f32)).astype(bf16)
+        MXS[lax.rem(u, 5)] = (MP[slot, 2 * c + xo].astype(f32) + MR1[j, xo].astype(f32)).astype(bf16)
         m2_copy(u, j).start()
         MR1[j, xx] = (MP[slot, 2 * c + xx].astype(f32) + MR1[j, xx].astype(f32)).astype(bf16)
         m1_copy(u, j).wait_send()
@@ -386,10 +378,20 @@
     def stage2(u):
         j = lax.rem(u, NJ)
         m2_copy(u, j).wait()
-        tot = (MR1[j, xx].astype(f32) + MR2[u].astype(f32)).astype(bf16).astype(f32)
+        tot = (MR1[j, xx].astype(f32) + MR2[j].astype(f32)).astype(bf16).astype(f32)
         gate, up = tot[0], tot[1]
-        AF[j, 2 * c + xx] = (gate * jax.nn.sigmoid(gate) * up).astype(bf16)
-        ax_copy(u, j).start()
+        act = (gate * jax.nn.sigmoid(gate) * up).astype(bf16)
+
+        @pl.when(u < NU - 1)
+        def _():
+            AF[j, 2 * c + xx] = act
+            ax_copy(u, j).start()
+
+        @pl.when(u == NU - 1)
+        def _():
+            AZ[2 * c + xx] = act
+            for k in (2, 1, 3):
+                az_copy(k).start()
 
     def stage3(u):
         j = lax.rem(u, NJ)
@@ -436,48 +438,22 @@
         def _():
             stage0(t)
 
-        @pl.when((t >= L1) & (t < NU + L1))
-        def _():
-            stage1(t - L1)
-
-        @pl.when((t >= L2) & (t < LATE))
-        def _():
-            stage2(t - L2)
-
-        @pl.when(t == NU)
-        def _():
-            lax.fori_loop(LATE - L2, NU - L2, lambda u, x: (stage2(u), x)[1], 0)
-
-        @pl.when((t >= NU) & (t < NU + L2))
-        def _():
-            stage2(t - L2)
-
-        @pl.when((t >= L3) & (t < LATE - L2 + L3))
-        def _():
-            stage3(t - L3)
-
-        @pl.when(t >= NU)
-        def _():
-            @pl.when(t < NU + LATE - L2)
-            def _():
-                stage3(t - (LATE - L2))
-
-        @pl.when((t >= L4) & (t < NU))
-        def _():
-            stage4(t - L4)
-
-        @pl.when(t > NU)
-        def _():
-            stage4(t - L4 - 1)
+        for lag, stage in ((L1, stage1), (L2, stage2), (L3, stage3), (L4, stage4)):
+            @pl.when((t >= lag) & (t < NU + lag - (lag >= L3)))
+            def _(lag=lag, stage=stage):
+                stage(t - lag)
 
         return carry
 
-    lax.fori_loop(0, NU + L4 + 1, step, 0)
+    lax.fori_loop(0, NU + L4 - 1, step, 0)
 
     h_store = pltpu.make_async_copy(HB.at[0], h_hbm, lsem.at[1])
     h_store.start()
     dy_copy().wait_recv()
-    mlp = (ACC[...] + DR[...].astype(f32)).astype(bf16)
+    for k in range(1, 4):
+        az_recv(k).wait_recv()
+    last = bdot(jnp.concatenate([AZ[b] for b in range(4)], axis=0), WB[(NJ - 1) * CH:NJ * CH, :])
+    mlp = (ACC[...] + last + DR[...].astype(f32)).astype(bf16)
     ay_copy(0, 0).wait_send()
     ay_copy(0, 1).wait_send()
     AO[0] = mlp
@@ -493,15 +469,16 @@
                 q2_copy(r, m).wait_send()
         if r == 1:
             q2_copy(1, 2, 1).wait_send()
-            for k in range(1, 4):
-                ob_copy(k).wait_send()
-        ox_copy(r).wait_send()
-        od_copy(r).wait_send()
+        for p in range(r + 1):
+            ox_copy(r, p).wait_send()
+            od_copy(r, p).wait_send()
         if r == 1:
             ay_copy(r, 0).wait_send()
             ay_copy(r, 1).wait_send()
         st2_all(r).wait_send()
     dy_copy().wait_send()
+    for k in range(1, 4):
+        az_copy(k).wait_send()
     h_store.wait()
     m_store.wait()
 
@@ -528,9 +505,10 @@
         vm((2, S, D1), bf16),
         vm((NP, 4, 2, 16, CH), bf16),
         vm((NJ, 2, 2, 16, CH), bf16),
+        vm((5, 2, 16, CH), bf16),
         vm((NJ, 2, 16, CH), bf16),
-        vm((NU, 2, 16, CH), bf16),
         vm((NJ, 4, 16, CH), bf16),
+        vm((4, 16, CH), bf16),
         vm((S, D1), f32),
         vm((S, D1), bf16),
         vm((S, D1), bf16),
@@ -540,9 +518,9 @@
         dma((9,)), dma((3,)), dma((1,)), dma((1,)),
         dma((2,)), dma((2,)), dma((2,)), dma((2,)),
         dma((3,)), dma((2, 3)), dma((4,)), dma((7,)),
-        dma((2,)), dma((2,)), dma((2,)), dma((2,)), dma((3,)), dma((3,)), dma((2, 2)), dma((2, 2)),
-        dma((NP,)), dma((5,)), dma((NJ,)), dma((NU,)),
-        dma((NJ,)), dma((NJ,)), dma((3,)), dma((NJ,)), dma((1,)), dma((1,)),
+        dma((3,)), dma((3,)), dma((3,)), dma((3,)), dma((2, 2)), dma((2, 2)),
+        dma((NP,)), dma((5,)), dma((5,)), dma((NJ,)),
+        dma((4,)), dma((NJ,)), dma((3,)), dma((NJ,)), dma((3,)), dma((3,)), dma((1,)), dma((1,)),
     ]
     h, mlp = pl.pallas_call(
         kernel,

time: 72.5 us -> 69.5 us (0.959)
  Pallas kernels: 70.7 us -> 67.7 us
    pallas_call x1, Pallas kernels: 70.7 us -> 67.7 us  [layer_fn(): pl.pallas_call(kernel, out_shape=[jax.ShapeDtypeStruct((S, D1), bf16)] *...]
where the time goes in v8:
time: 69.5 us; the launch traced here: 69.4 us
  Pallas kernels  67.7 us (97%)
  other arithmetic  1.7 us (2%)
    pallas_call x1, Pallas kernels, layer_fn(): pl.pallas_call(kernel, out_shape=[jax.ShapeDtypeStruct((S, D1), bf16)] *...  67.7 us
    reshape x1, other arithmetic, layer_fn(): return (h.astype(f32) + mlp.astype(f32)).astype(bf16).reshape(x_blk.shape)  1.7 us

profile of v8, /device:TPU:0, one launch (start us, length us, event | category | flops | bytes accessed | tf_op | source)
XLA Modules:
  0.0 69.4 jit_solution(12858821063586580018)
XLA Ops:
  0.0 67.7 %shard_map.100 = (bf16[64,1280]{1,0:T(8,128)(2,1)}, bf16[64,1280]{1,0:T(8,128)(2,1)}) custom-call(bf16[64,1280]{1,0:T(8,128)(2,1)} %bitcast.3, bf16[1280,2560]{1,0:T(8,128)(2,1)} %wq.1, bf16[1280,2560]{1,0:T(8,128)(2,1)} %wk.1, bf16[1280,2560]{1,0:T(8,128)(2,1)} %wv.1, bf16[2560,1280]{1,0:T(8,128)(2,1)} %wo.1, bf16[1280,6912]{1,0:T(8,128)(2,1)} %wg.1, ...), custom_call_target="tpu_custom_call" | custom-call | tf_op jit(solution)/shard_map/pallas_call | solution.py:525
  67.7 1.7 %fusion = bf16[1,64,1280]{2,1,0:T(8,128)(2,1)} fusion(bf16[64,1280]{1,0:T(8,128)(2,1)} %get-tuple-element.8, bf16[64,1280]{1,0:T(8,128)(2,1)} %get-tuple-element.7), kind=kLoop, calls=%fused_computation.1 | loop fusion | flops 327680 | bytes 491520 | tf_op jit(solution)/shard_map/reshape | solution.py:533

commit v9 on v8

--- a/solution.py
+++ b/solution.py
@@ -44,8 +44,8 @@
     WA, WB, XB, NB, HB, ST1, ST2, PS, PO, R1, XS, R2, OF, AO, AR,
     MP, MR1, MXS, MR2, AF, AZ, ACC, DS, DR, COS, SIN, PR,
     wsem, lsem, xg_s, xg_r, st1_s, st1_r, st2_s, st2_r,
-    q1_s, q1_r, q2_s, q2_r, ox_s, ox_r, od_s, od_r, ay_s, ay_r,
-    m1_s, m1_r, m2_s, m2_r, ax_s, ax_r, ad_s, ad_r, az_s, az_r, dy_s, dy_r,
+    q1_s, q1_r, q2_s, q2_r, ox_s, ox_r, od_s, od_r, oe_s, oe_r, ay_s, ay_r,
+    az_s, az_r, dy_s, dy_r,
 ):
     f32, bf16 = jnp.float32, jnp.bfloat16
     ty = lax.axis_index("ty")
@@ -136,7 +136,7 @@
     x_send.start()
 
     def q1_copy(r, m):
-        return rcopy(PS.at[m], R1.at[r, m], q1_s.at[m], q1_r.at[r, m], partner)
+        return rcopy(PS.at[m], R1.at[r, m], q1_s.at[m], q1_r.at[3 * r + m], partner)
 
     def q2_copy(r, m, p=0):
         lanes = pl.ds(*(PARTS[p] if r == 1 and m == 2 else (0, GW)))
@@ -190,12 +190,18 @@
         return rcopy(ref, ref, ox_s.at[r + p], ox_r.at[r + p], xpeer)
 
     def od_copy(r, p=0):
-        ref = OF.at[r, c, :, :, o_lanes(r, p)]
+        ref = OF.at[r, c, xo, :, o_lanes(r, p)]
         return rcopy(ref, ref, od_s.at[r + p], od_r.at[r + p], partner)
 
     def od_recv(r, p=0):
-        ref = OF.at[r, co, :, :, o_lanes(r, p)]
+        ref = OF.at[r, co, xo, :, o_lanes(r, p)]
         return rcopy(ref, ref, od_s.at[r + p], od_r.at[r + p], partner)
+
+    def oe_copy(r):
+        return rcopy(OF.at[r, c, xx], OF.at[r, c, xx], oe_s.at[r], oe_r.at[r], partner)
+
+    def oe_recv(r):
+        return rcopy(OF.at[r, co, xx], OF.at[r, co, xx], oe_s.at[r], oe_r.at[r], partner)
 
     def total(r, m, lanes):
         return (PO[r, m, xx, :, lanes].astype(f32) + R1[r, m, xx, :, lanes].astype(f32) + R2[r, m, :, lanes].astype(f32)).astype(bf16)
@@ -226,6 +232,8 @@
         outs = [bdot(PR[h], total(r, 2, pl.ds(h * HEAD_DIM, HEAD_DIM))).astype(bf16) for h in heads]
         OF[r, c, xx, :, off:off + size] = jnp.concatenate(outs, axis=1)
         ox_copy(r, p).start()
+        if r == 0 or p == 1:
+            oe_copy(r).start()
 
     def o_forward(r, p=0):
         ox_recv(r, p).wait_recv()
@@ -235,25 +243,19 @@
         cols = pl.ds(*((0, CH), (CH, D1 - CH))[p])
         return rcopy(AO.at[r, :, cols], AR.at[1 - r, :, cols], ay_s.at[r, p], ay_r.at[1 - r, p], ypeer)
 
-    def heads_of(r, half):
-        return jnp.concatenate([OF[r, half, 0], OF[r, half, 1]], axis=1)
-
-    def out_own(r):
-        if r == 0:
-            await_all(WA.at[pl.ds(14, 2)], 3)
-            await_all(WA.at[pl.ds(16, 2), :, pl.ds(0, D1 - CH)], 4)
-        o = heads_of(r, c)
-        ACC[:, :CH] = bdot(o, WA[14 + c])
-        ACC[:, CH:] = bdot(o, WA[16 + c, :, : D1 - CH])
-
-    def out_rest(r):
+    def out_block(r, cb, xb, first=False):
+        o, rows = OF[r, cb, xb], pl.ds(pl.multiple_of(xb * GW, GW), GW)
+        for cols, prod in ((slice(0, CH), bdot(o, WA[14 + cb, rows, :])), (slice(CH, D1), bdot(o, WA[16 + cb, rows, : D1 - CH]))):
+            ACC[:, cols] = prod if first else ACC[:, cols] + prod
+
+    def out_last(r):
         od_recv(r).wait_recv()
         if r == 1:
             od_recv(r, 1).wait_recv()
-        o = heads_of(r, co)
-        AO[r, :, :CH] = (ACC[:, :CH] + bdot(o, WA[14 + co])).astype(bf16)
+        o, rows = OF[r, co, xo], pl.ds(pl.multiple_of(xo * GW, GW), GW)
+        AO[r, :, :CH] = (ACC[:, :CH] + bdot(o, WA[14 + co, rows, :])).astype(bf16)
         ay_copy(r, 0).start()
-        AO[r, :, CH:] = (ACC[:, CH:] + bdot(o, WA[16 + co, :, : D1 - CH])).astype(bf16)
+        AO[r, :, CH:] = (ACC[:, CH:] + bdot(o, WA[16 + co, rows, : D1 - CH])).astype(bf16)
         ay_copy(r, 1).start()
 
     st1_all().wait_recv()
@@ -284,16 +286,24 @@
     qkv_mm_both(1, 2)
     wd_load().start()
     qkv_s1(1, 2)
+    await_all(WA.at[pl.ds(14, 2)], 3)
+    await_all(WA.at[pl.ds(16, 2), :, pl.ds(0, D1 - CH)], 4)
+    out_block(0, c, xx, True)
     o_forward(0)
-    out_own(0)
-    out_rest(0)
+    oe_recv(0).wait_recv()
+    out_block(0, co, xx)
+    out_block(0, c, xo)
+    out_last(0)
     scores(1)
     values(1, 0)
     values(1, 1)
+    out_block(1, c, xx, True)
+    oe_recv(1).wait_recv()
+    out_block(1, co, xx)
     o_forward(1, 0)
     o_forward(1, 1)
-    out_own(1)
-    out_rest(1)
+    out_block(1, c, xo)
+    out_last(1)
     for j in range(7, NJ):
         gu_load(j, 0).start()
         gu_load(j, 1).start()
@@ -320,25 +330,34 @@
         NB[r] = normalize(HB[r].astype(f32), ST2[r, 0] + ST2[r, 1] + ST2[r, 2] + ST2[r, 3])
 
     residual(1)
+    for m in range(3):
+        q1_copy(1, m).wait_send()
+        q2_copy(1, m).wait_send()
+    q2_copy(1, 2, 1).wait_send()
+    for r, p in ((0, 0), (1, 0), (1, 1)):
+        ox_copy(r, p).wait_send()
+        od_copy(r, p).wait_send()
+    for r in range(2):
+        oe_copy(r).wait_send()
     norm2(1)
 
     def m1_copy(u, j):
-        return rcopy(MP.at[lax.rem(u, NP), pl.ds(2 * co, 2)], MR1.at[j], m1_s.at[lax.rem(u, NP)], m1_r.at[lax.rem(u, 5)], partner)
+        return rcopy(MP.at[lax.rem(u, NP), pl.ds(2 * co, 2)], MR1.at[j], q1_s.at[lax.rem(u, NP)], q1_r.at[lax.rem(u, 5)], partner)
 
     def m2_copy(u, j):
-        return rcopy(MXS.at[lax.rem(u, 5)], MR2.at[j], m2_s.at[lax.rem(u, 5)], m2_r.at[j], xpeer)
+        return rcopy(MXS.at[lax.rem(u, 5)], MR2.at[j], q2_s.at[lax.rem(u, 5)], q2_r.at[j], xpeer)
 
     def ax_copy(u, j):
-        return rcopy(AF.at[j, 2 * c + xx], AF.at[j, 2 * c + xx], ax_s.at[lax.rem(u, 4)], ax_r.at[j], xpeer)
+        return rcopy(AF.at[j, 2 * c + xx], AF.at[j, 2 * c + xx], ox_s.at[lax.rem(u, 4)], ox_r.at[j], xpeer)
 
     def ax_recv(u, j):
-        return rcopy(AF.at[j, 2 * c + xo], AF.at[j, 2 * c + xo], ax_s.at[lax.rem(u, 4)], ax_r.at[j], xpeer)
+        return rcopy(AF.at[j, 2 * c + xo], AF.at[j, 2 * c + xo], ox_s.at[lax.rem(u, 4)], ox_r.at[j], xpeer)
 
     def ad_copy(u, j):
-        return rcopy(AF.at[j, pl.ds(2 * c, 2)], AF.at[j, pl.ds(2 * c, 2)], ad_s.at[lax.rem(u, 3)], ad_r.at[j], partner)
+        return rcopy(AF.at[j, pl.ds(2 * c, 2)], AF.at[j, pl.ds(2 * c, 2)], od_s.at[lax.rem(u, 3)], od_r.at[j], partner)
 
     def ad_recv(u, j):
-        return rcopy(AF.at[j, pl.ds(2 * co, 2)], AF.at[j, pl.ds(2 * co, 2)], ad_s.at[lax.rem(u, 3)], ad_r.at[j], partner)
+        return rcopy(AF.at[j, pl.ds(2 * co, 2)], AF.at[j, pl.ds(2 * co, 2)], od_s.at[lax.rem(u, 3)], od_r.at[j], partner)
 
     def az_copy(k):
         return rcopy(AZ.at[2 * c + xx], AZ.at[2 * c + xx], az_s.at[k - 1], az_r.at[k - 1], {"tx": lax.rem(tx + k, 4)})
@@ -462,19 +481,9 @@
     st1_all().wait_send()
     st1_total().wait_send()
     x_send.wait_send()
+    ay_copy(1, 0).wait_send()
+    ay_copy(1, 1).wait_send()
     for r in range(2):
-        for m in range(3):
-            if r == 1:
-                q1_copy(r, m).wait_send()
-                q2_copy(r, m).wait_send()
-        if r == 1:
-            q2_copy(1, 2, 1).wait_send()
-        for p in range(r + 1):
-            ox_copy(r, p).wait_send()
-            od_copy(r, p).wait_send()
-        if r == 1:
-            ay_copy(r, 0).wait_send()
-            ay_copy(r, 1).wait_send()
         st2_all(r).wait_send()
     dy_copy().wait_send()
     for k in range(1, 4):
@@ -517,10 +526,9 @@
         vm((GH, S, S), bf16),
         dma((9,)), dma((3,)), dma((1,)), dma((1,)),
         dma((2,)), dma((2,)), dma((2,)), dma((2,)),
-        dma((3,)), dma((2, 3)), dma((4,)), dma((7,)),
-        dma((3,)), dma((3,)), dma((3,)), dma((3,)), dma((2, 2)), dma((2, 2)),
-        dma((NP,)), dma((5,)), dma((5,)), dma((NJ,)),
-        dma((4,)), dma((NJ,)), dma((3,)), dma((NJ,)), dma((3,)), dma((3,)), dma((1,)), dma((1,)),
+        dma((3,)), dma((6,)), dma((5,)), dma((NJ,)),
+        dma((4,)), dma((NJ,)), dma((3,)), dma((NJ,)), dma((2,)), dma((2,)), dma((2, 2)), dma((2, 2)),
+        dma((3,)), dma((3,)), dma((1,)), dma((1,)),
     ]
     h, mlp = pl.pallas_call(
         kernel,

time: 69.5 us -> 68.5 us (0.986)
  Pallas kernels: 67.7 us -> 66.7 us
    pallas_call x1, Pallas kernels: 67.7 us -> 66.7 us  [layer_fn(): pl.pallas_call(kernel, out_shape=[jax.ShapeDtypeStruct((S, D1), bf16)] *...]
where the time goes in v9:
time: 68.5 us; the launch traced here: 68.4 us
  Pallas kernels  66.7 us (97%)
  other arithmetic  1.7 us (2%)
    pallas_call x1, Pallas kernels, layer_fn(): pl.pallas_call(kernel, out_shape=[jax.ShapeDtypeStruct((S, D1), bf16)] *...  66.7 us
    reshape x1, other arithmetic, layer_fn(): return (h.astype(f32) + mlp.astype(f32)).astype(bf16).reshape(x_blk.shape)  1.7 us

profile of v9, /device:TPU:0, one launch (start us, length us, event | category | flops | bytes accessed | tf_op | source)
XLA Modules:
  0.0 68.4 jit_solution(11469620528986147908)
XLA Ops:
  0.0 66.7 %shard_map.100 = (bf16[64,1280]{1,0:T(8,128)(2,1)}, bf16[64,1280]{1,0:T(8,128)(2,1)}) custom-call(bf16[64,1280]{1,0:T(8,128)(2,1)} %bitcast.3, bf16[1280,2560]{1,0:T(8,128)(2,1)} %wq.1, bf16[1280,2560]{1,0:T(8,128)(2,1)} %wk.1, bf16[1280,2560]{1,0:T(8,128)(2,1)} %wv.1, bf16[2560,1280]{1,0:T(8,128)(2,1)} %wo.1, bf16[1280,6912]{1,0:T(8,128)(2,1)} %wg.1, ...), custom_call_target="tpu_custom_call" | custom-call | tf_op jit(solution)/shard_map/pallas_call | solution.py:533
  66.7 1.7 %fusion = bf16[1,64,1280]{2,1,0:T(8,128)(2,1)} fusion(bf16[64,1280]{1,0:T(8,128)(2,1)} %get-tuple-element.8, bf16[64,1280]{1,0:T(8,128)(2,1)} %get-tuple-element.7), kind=kLoop, calls=%fused_computation.1 | loop fusion | flops 327680 | bytes 491520 | tf_op jit(solution)/shard_map/reshape | solution.py:541

commit v10 on v9

--- a/solution.py
+++ b/solution.py
@@ -23,7 +23,7 @@
 NU = 2 * NJ
 NP = 3
 PARTS = ((0, 384), (384, 256))
-L1, L2, L3, L4 = 1, 4, 7, 9
+L1, L2, L3, L4 = 1, 4, 6, 8
 
 
 def rotary_tables():
@@ -40,7 +40,7 @@
 
 
 def kernel(
-    x_hbm, wq, wk, wv, wo, wg, wu, wd, cos_hbm, sin_hbm, h_hbm, m_hbm,
+    x_hbm, wq, wk, wv, wo, wg, wu, wd, cos_hbm, sin_hbm, y_hbm,
     WA, WB, XB, NB, HB, ST1, ST2, PS, PO, R1, XS, R2, OF, AO, AR,
     MP, MR1, MXS, MR2, AF, AZ, ACC, DS, DR, COS, SIN, PR,
     wsem, lsem, xg_s, xg_r, st1_s, st1_r, st2_s, st2_r,
@@ -466,8 +466,6 @@
 
     lax.fori_loop(0, NU + L4 - 1, step, 0)
 
-    h_store = pltpu.make_async_copy(HB.at[0], h_hbm, lsem.at[1])
-    h_store.start()
     dy_copy().wait_recv()
     for k in range(1, 4):
         az_recv(k).wait_recv()
@@ -475,9 +473,9 @@
     mlp = (ACC[...] + last + DR[...].astype(f32)).astype(bf16)
     ay_copy(0, 0).wait_send()
     ay_copy(0, 1).wait_send()
-    AO[0] = mlp
-    m_store = pltpu.make_async_copy(AO.at[0], m_hbm, lsem.at[0])
-    m_store.start()
+    AO[0] = (HB[0].astype(f32) + mlp.astype(f32)).astype(bf16)
+    y_store = pltpu.make_async_copy(AO.at[0], y_hbm, lsem.at[0])
+    y_store.start()
     st1_all().wait_send()
     st1_total().wait_send()
     x_send.wait_send()
@@ -488,8 +486,7 @@
     dy_copy().wait_send()
     for k in range(1, 4):
         az_copy(k).wait_send()
-    h_store.wait()
-    m_store.wait()
+    y_store.wait()
 
 
 def layer_fn(x_blk, w_q, w_k, w_v, w_o, w_gate, w_up, w_down):
@@ -530,15 +527,15 @@
         dma((4,)), dma((NJ,)), dma((3,)), dma((NJ,)), dma((2,)), dma((2,)), dma((2, 2)), dma((2, 2)),
         dma((3,)), dma((3,)), dma((1,)), dma((1,)),
     ]
-    h, mlp = pl.pallas_call(
+    y = pl.pallas_call(
         kernel,
-        out_shape=[jax.ShapeDtypeStruct((S, D1), bf16)] * 2,
+        out_shape=jax.ShapeDtypeStruct((S, D1), bf16),
         in_specs=[pl.BlockSpec(memory_space=pl.ANY)] * 10,
-        out_specs=[pl.BlockSpec(memory_space=pl.ANY)] * 2,
+        out_specs=pl.BlockSpec(memory_space=pl.ANY),
         scratch_shapes=scratch,
         compiler_params=pltpu.CompilerParams(collective_id=0, has_side_effects=True, vmem_limit_bytes=67_043_328),
     )(x_blk.reshape(S, D1), w_q, w_k, w_v, w_o, w_gate, w_up, w_down, jnp.asarray(cos_t), jnp.asarray(sin_t))
-    return (h.astype(f32) + mlp.astype(f32)).astype(bf16).reshape(x_blk.shape)
+    return y.reshape(x_blk.shape)
 
 
 def solution(mesh):

time: 68.5 us -> 69.9 us (1.020)
  other arithmetic: 1.7 us -> 0 us
  local copies, waits for them, and re-layouts: 0 us -> 1.59 us
  Pallas kernels: 66.7 us -> 68.2 us
    reshape x1 -> x0, other arithmetic: 1.7 us -> none  [layer_fn(): return (h.astype(f32) + mlp.astype(f32)).astype(bf16).reshape(x_blk.shape)]
    unnamed x0 -> x1, local copies, waits for them, and re-layouts: none -> 1.59 us
    pallas_call x1, Pallas kernels: 66.7 us -> 68.2 us  [layer_fn(): pl.pallas_call(kernel, out_shape=jax.ShapeDtypeStruct((S, D1), bf16), in_...]
where the time goes in v10:
time: 69.9 us; the launch traced here: 69.8 us
  Pallas kernels  68.2 us (98%)
  local copies, waits for them, and re-layouts  1.59 us (2%)
    pallas_call x1, Pallas kernels, layer_fn(): pl.pallas_call(kernel, out_shape=jax.ShapeDtypeStruct((S, D1), bf16), in_...  68.2 us
    unnamed x1, local copies, waits for them, and re-layouts  1.59 us

profile of v10, /device:TPU:0, one launch (start us, length us, event | category | flops | bytes accessed | tf_op | source)
XLA Modules:
  0.0 69.8 jit_solution(7865198438263312365)
XLA Ops:
  0.0 68.2 %shard_map.100 = bf16[64,1280]{1,0:T(8,128)(2,1)} custom-call(bf16[64,1280]{1,0:T(8,128)(2,1)} %bitcast.3, bf16[1280,2560]{1,0:T(8,128)(2,1)} %wq.1, bf16[1280,2560]{1,0:T(8,128)(2,1)} %wk.1, bf16[1280,2560]{1,0:T(8,128)(2,1)} %wv.1, bf16[2560,1280]{1,0:T(8,128)(2,1)} %wo.1, bf16[1280,6912]{1,0:T(8,128)(2,1)} %wg.1, bf16[1280,6912]{1,0:T(8,128)(2,1)} %wu.1, ...), custom_call_target="tpu_custom_call" | custom-call | tf_op jit(solution)/shard_map/pallas_call | solution.py:530
  68.2 1.6 %copy.12 = bf16[1,64,1280]{2,1,0:T(8,128)(2,1)} copy(bf16[1,64,1280]{2,1,0:T(8,128)(2,1)} %bitcast.2) | data formatting | bytes 327680

commit v11 on v10

--- a/solution.py
+++ b/solution.py
@@ -23,7 +23,8 @@
 NU = 2 * NJ
 NP = 3
 PARTS = ((0, 384), (384, 256))
-L1, L2, L3, L4 = 1, 4, 6, 8
+NA = 11
+L1, L2, L3, L4 = 1, 4, 8, 10
 
 
 def rotary_tables():
@@ -348,16 +349,16 @@
         return rcopy(MXS.at[lax.rem(u, 5)], MR2.at[j], q2_s.at[lax.rem(u, 5)], q2_r.at[j], xpeer)
 
     def ax_copy(u, j):
-        return rcopy(AF.at[j, 2 * c + xx], AF.at[j, 2 * c + xx], ox_s.at[lax.rem(u, 4)], ox_r.at[j], xpeer)
+        return rcopy(AF.at[lax.rem(u, NA), 2 * c + xx], AF.at[lax.rem(u, NA), 2 * c + xx], ox_s.at[lax.rem(u, 5)], ox_r.at[j], xpeer)
 
     def ax_recv(u, j):
-        return rcopy(AF.at[j, 2 * c + xo], AF.at[j, 2 * c + xo], ox_s.at[lax.rem(u, 4)], ox_r.at[j], xpeer)
+        return rcopy(AF.at[lax.rem(u, NA), 2 * c + xo], AF.at[lax.rem(u, NA), 2 * c + xo], ox_s.at[lax.rem(u, 5)], ox_r.at[j], xpeer)
 
     def ad_copy(u, j):
-        return rcopy(AF.at[j, pl.ds(2 * c, 2)], AF.at[j, pl.ds(2 * c, 2)], od_s.at[lax.rem(u, 3)], od_r.at[j], partner)
+        return rcopy(AF.at[lax.rem(u, NA), pl.ds(2 * c, 2)], AF.at[lax.rem(u, NA), pl.ds(2 * c, 2)], od_s.at[lax.rem(u, 3)], od_r.at[j], partner)
 
     def ad_recv(u, j):
-        return rcopy(AF.at[j, pl.ds(2 * co, 2)], AF.at[j, pl.ds(2 * co, 2)], od_s.at[lax.rem(u, 3)], od_r.at[j], partner)
+        return rcopy(AF.at[lax.rem(u, NA), pl.ds(2 * co, 2)], AF.at[lax.rem(u, NA), pl.ds(2 * co, 2)], od_s.at[lax.rem(u, 3)], od_r.at[j], partner)
 
     def az_copy(k):
         return rcopy(AZ.at[2 * c + xx], AZ.at[2 * c + xx], az_s.at[k - 1], az_r.at[k - 1], {"tx": lax.rem(tx + k, 4)})
@@ -403,7 +404,7 @@
 
         @pl.when(u < NU - 1)
         def _():
-            AF[j, 2 * c + xx] = act
+            AF[lax.rem(u, NA), 2 * c + xx] = act
             ax_copy(u, j).start()
 
         @pl.when(u == NU - 1)
@@ -426,7 +427,7 @@
             wd_load().wait()
 
         ad_recv(u, j).wait_recv()
-        a = jnp.concatenate([AF[j, b] for b in range(4)], axis=0)
+        a = jnp.concatenate([AF[lax.rem(u, NA), b] for b in range(4)], axis=0)
         prod = bdot(a, WB[pl.ds(pl.multiple_of(j * CH, CH), CH), :])
 
         @pl.when(j == 0)
@@ -513,7 +514,7 @@
         vm((NJ, 2, 2, 16, CH), bf16),
         vm((5, 2, 16, CH), bf16),
         vm((NJ, 2, 16, CH), bf16),
-        vm((NJ, 4, 16, CH), bf16),
+        vm((NA, 4, 16, CH), bf16),
         vm((4, 16, CH), bf16),
         vm((S, D1), f32),
         vm((S, D1), bf16),
@@ -524,7 +525,7 @@
         dma((9,)), dma((3,)), dma((1,)), dma((1,)),
         dma((2,)), dma((2,)), dma((2,)), dma((2,)),
         dma((3,)), dma((6,)), dma((5,)), dma((NJ,)),
-        dma((4,)), dma((NJ,)), dma((3,)), dma((NJ,)), dma((2,)), dma((2,)), dma((2, 2)), dma((2, 2)),
+        dma((5,)), dma((NJ,)), dma((3,)), dma((NJ,)), dma((2,)), dma((2,)), dma((2, 2)), dma((2, 2)),
         dma((3,)), dma((3,)), dma((1,)), dma((1,)),
     ]
     y = pl.pallas_call(

time: 69.9 us -> 68.6 us (0.981)
  Pallas kernels: 68.2 us -> 66.9 us
    pallas_call x1, Pallas kernels: 68.2 us -> 66.9 us  [layer_fn(): pl.pallas_call(kernel, out_shape=jax.ShapeDtypeStruct((S, D1), bf16), in_...]
where the time goes in v11:
time: 68.6 us; the launch traced here: 68.5 us
  Pallas kernels  66.9 us (98%)
  local copies, waits for them, and re-layouts  1.59 us (2%)
    pallas_call x1, Pallas kernels, layer_fn(): pl.pallas_call(kernel, out_shape=jax.ShapeDtypeStruct((S, D1), bf16), in_...  66.9 us
    unnamed x1, local copies, waits for them, and re-layouts  1.59 us

profile of v11, /device:TPU:0, one launch (start us, length us, event | category | flops | bytes accessed | tf_op | source)
XLA Modules:
  0.0 68.5 jit_solution(12825976720079818780)
XLA Ops:
  0.0 66.9 %shard_map.100 = bf16[64,1280]{1,0:T(8,128)(2,1)} custom-call(bf16[64,1280]{1,0:T(8,128)(2,1)} %bitcast.3, bf16[1280,2560]{1,0:T(8,128)(2,1)} %wq.1, bf16[1280,2560]{1,0:T(8,128)(2,1)} %wk.1, bf16[1280,2560]{1,0:T(8,128)(2,1)} %wv.1, bf16[2560,1280]{1,0:T(8,128)(2,1)} %wo.1, bf16[1280,6912]{1,0:T(8,128)(2,1)} %wg.1, bf16[1280,6912]{1,0:T(8,128)(2,1)} %wu.1, ...), custom_call_target="tpu_custom_call" | custom-call | tf_op jit(solution)/shard_map/pallas_call | solution.py:531
  66.9 1.6 %copy.12 = bf16[1,64,1280]{2,1,0:T(8,128)(2,1)} copy(bf16[1,64,1280]{2,1,0:T(8,128)(2,1)} %bitcast.2) | data formatting | bytes 327680
